TPU v7x, 32 devices: a whole 2x2x4 slice. The times are simulated.
32 devices in a mesh: rep: 8 (over z, x), ep: 4 (over y, core).
Axes of the slice: x: 2, y: 2, z: 4, core: 2. Of those that a mesh axis runs over, the one named last changes fastest.
Arguments:
- tokens: bfloat16 [6144, 2048], P(('rep', 'ep')), may hold values from -6 to 6
- upstream: bfloat16 [6144, 2048], P(('rep', 'ep')), may hold values from -3 to 3
- route_ids: int32 [6144, 2], P(('rep', 'ep')), may hold values from 0 to 3, all different within a row; in each aligned block of 192 rows (0 to 191, 192 to 383, ...) at most 144 rows name the same one
- route_probs: bfloat16 [6144, 2], P(('rep', 'ep')), may hold values from 0.19921875 to 1
- gate_proj: bfloat16 [4, 2048, 768], P('ep'), may hold values from -0.125 to 0.125
- up_proj: bfloat16 [4, 2048, 768], P('ep'), may hold values from -0.125 to 0.125
- down_proj: bfloat16 [4, 768, 2048], P('ep'), may hold values from -0.21875 to 0.21875
Outputs:
- grad_tokens: bfloat16 [6144, 2048], P(('rep', 'ep'))
- grad_probs: bfloat16 [6144, 2], P(('rep', 'ep'))
- grad_gate: float32 [4, 2048, 768], P('ep', 'rep')
- grad_up: float32 [4, 2048, 768], P('ep', 'rep')
- grad_down: float32 [4, 768, 2048], P('ep', None, 'rep')
Inputs may be any that keep to these rules, and one draw needn't show every extreme that they name: `route_ids`: each row names 2 different experts. Among the rows of one device no expert is named more than 144 times, and in every draw some expert is named exactly 144 times by the rows of some device.
All inputs are finite; a program needn't handle non-finite values.
Results may differ from a plain program's by a relative error of at most 0.0058.
Values may be sent and summed in bfloat16 or wider, within the bound.
No kernel may reach another device: no remote copies, remote signals or barrier semaphores. Data moves between devices by JAX's collectives and lax.ppermute only.
A program may use at most 128 MiB of HBM per device.

v0:
```python
import jax
import jax.numpy as jnp
from jax import lax
from jax.sharding import PartitionSpec as P


def place_routes(route_block, expert_total, capacity):
    flat_ids = route_block.reshape(-1)
    onehot = (flat_ids[:, None] == jnp.arange(expert_total, dtype=jnp.int32)[None, :]).astype(
        jnp.int32
    )
    before = jnp.cumsum(onehot, axis=0) - onehot
    slot_index = jnp.sum(before * onehot, axis=1)
    target = flat_ids * capacity + slot_index
    route_total = flat_ids.shape[0]
    source = (
        jnp.zeros((expert_total * capacity,), jnp.int32)
        .at[target]
        .set(jnp.arange(route_total, dtype=jnp.int32))
    )
    filled = (
        jnp.zeros((expert_total * capacity,), jnp.int32)
        .at[target]
        .set(jnp.ones((route_total,), jnp.int32))
    )
    return (target, source, filled)


def expert_backward(expert_in, expert_up, expert_prob, gate_weight, up_weight, down_weight):
    gate_act = jnp.dot(expert_in, gate_weight, preferred_element_type=jnp.float32)
    up_act = jnp.dot(expert_in, up_weight, preferred_element_type=jnp.float32)
    sigmoid_gate = jax.nn.sigmoid(gate_act)
    silu_gate = gate_act * sigmoid_gate
    activation = silu_gate * up_act
    back_proj = lax.dot_general(
        expert_up, down_weight, (((1,), (1,)), ((), ())), preferred_element_type=jnp.float32
    )
    prob_grad = jnp.sum(activation * back_proj, axis=1).astype(jnp.bfloat16)
    prob_col = expert_prob.astype(jnp.float32)[:, None]
    weighted = (prob_col * activation).astype(jnp.bfloat16)
    act_grad = prob_col * back_proj
    gate_grad = (act_grad * up_act * sigmoid_gate * (1.0 + gate_act * (1.0 - sigmoid_gate))).astype(
        jnp.bfloat16
    )
    up_grad = (act_grad * silu_gate).astype(jnp.bfloat16)
    routed = lax.dot_general(
        gate_grad, gate_weight, (((1,), (1,)), ((), ())), preferred_element_type=jnp.float32
    )
    routed = routed + lax.dot_general(
        up_grad, up_weight, (((1,), (1,)), ((), ())), preferred_element_type=jnp.float32
    )
    return (gate_grad, up_grad, weighted, routed.astype(jnp.bfloat16), prob_grad)


def body(tokens, upstream, route_ids, route_probs, gate_proj, up_proj, down_proj):
    ep_count = lax.axis_size("ep")
    rep_count = lax.axis_size("rep")
    tok_rows, model_width = tokens.shape
    fanout = route_ids.shape[1]
    hidden = gate_proj.shape[2]
    capacity = 3 * tok_rows * fanout // (2 * ep_count)
    target, source, filled = place_routes(route_ids, ep_count, capacity)
    owner_row = source // fanout
    keep_mask = filled.astype(jnp.bfloat16)
    send_in = (tokens[owner_row] * keep_mask[:, None]).reshape(ep_count, capacity, model_width)
    send_up = (upstream[owner_row] * keep_mask[:, None]).reshape(ep_count, capacity, model_width)
    send_prob = (route_probs.reshape(-1)[source] * keep_mask).reshape(ep_count, capacity)
    recv_in, recv_up, recv_prob = (
        lax.all_to_all(send_in, "ep", split_axis=0, concat_axis=0, tiled=True),
        lax.all_to_all(send_up, "ep", split_axis=0, concat_axis=0, tiled=True),
        lax.all_to_all(send_prob, "ep", split_axis=0, concat_axis=0, tiled=True),
    )
    slot_rows = ep_count * capacity
    expert_in = recv_in.reshape(slot_rows, model_width)
    expert_up = recv_up.reshape(slot_rows, model_width)
    expert_prob = recv_prob.reshape(slot_rows)
    gate_grad, up_grad, weighted, routed, prob_grad = expert_backward(
        expert_in, expert_up, expert_prob, gate_proj[0], up_proj[0], down_proj[0]
    )
    return_rows, return_probs = (
        lax.all_to_all(
            routed.reshape(ep_count, capacity, model_width),
            "ep",
            split_axis=0,
            concat_axis=0,
            tiled=True,
        ),
        lax.all_to_all(
            prob_grad.reshape(ep_count, capacity), "ep", split_axis=0, concat_axis=0, tiled=True
        ),
    )
    route_rows = return_rows.reshape(slot_rows, model_width)[target]
    grad_tokens = jnp.sum(
        route_rows.reshape(tok_rows, fanout, model_width), axis=1, dtype=jnp.float32
    ).astype(jnp.bfloat16)
    grad_probs = return_probs.reshape(-1)[target].reshape(tok_rows, fanout)
    rescale = 1.0 / rep_count
    pair_grad = jnp.concatenate([gate_grad, up_grad], axis=1)
    contract = (((0,), (0,)), ((), ()))
    reduced = (
        lax.psum_scatter(
            lax.dot_general(expert_in, pair_grad, contract, preferred_element_type=jnp.float32),
            "rep",
            scatter_dimension=0,
            tiled=True,
        )
        * rescale
    )
    grad_gate = reduced[:, :hidden]
    grad_up = reduced[:, hidden:]
    down_term = lax.dot_general(weighted, expert_up, contract, preferred_element_type=jnp.float32)
    grad_down = lax.psum_scatter(down_term, "rep", scatter_dimension=1, tiled=True) * rescale
    return (grad_tokens, grad_probs, grad_gate[None], grad_up[None], grad_down[None])


def solution(mesh):
    return jax.shard_map(
        body,
        mesh=mesh,
        in_specs=(
            P(("rep", "ep"), None),
            P(("rep", "ep"), None),
            P(("rep", "ep"), None),
            P(("rep", "ep"), None),
            P("ep", None, None),
            P("ep", None, None),
            P("ep", None, None),
        ),
        out_specs=(
            P(("rep", "ep"), None),
            P(("rep", "ep"), None),
            P("ep", "rep", None),
            P("ep", "rep", None),
            P("ep", None, "rep"),
        ),
        check_vma=False,
    )
```

profile of v0, /device:TPU:0, one launch (start us, length us, event | category | flops | bytes accessed | tf_op | source)
XLA Modules:
  0.0 461.7 jit_solution(995768127440423109)
XLA Ops:
  7.2 0.8 broadcast_multiply_fusion.3
  8.0 0.9 copy.19
  8.9 0.1 eq.29
  9.1 0.1 eq.25
  9.2 0.8 copy.17
  10.0 0.2 reshape.123
  10.2 0.1 copy.18
  10.3 0.1 mul.92
  10.5 1.2 reduce-window.6
  11.7 0.2 slice_reduce_fusion
  11.9 0.2 reduce-window.9
  12.3 2.9 scatter_custom_fusion.1
  15.2 2.9 scatter_custom_fusion
  18.2 3.9 gather_fusion
  22.1 0.7 all_to_all.25
  22.8 4.3 all-to-all-start
  27.2 8.1 %gather_fusion.2 = bf16[576,2048]{1,0:T(8,128)(2,1)} fusion(bf16[192,2048]{1,0:T(8,128)(2,1)} %param.7, s32[1024]{0:T(1024)S(1)} %get-tuple-element.26), kind=kCustom, calls=%fused_computation.2 | custom fusion | bytes 4720896 | tf_op jit(solution)/shard_map/gather | solution.py:65
  35.2 8.1 %gather_fusion.1 = bf16[576,2048]{1,0:T(8,128)(2,1)} fusion(bf16[192,2048]{1,0:T(8,128)(2,1)} %param.8, s32[1024]{0:T(1024)S(1)} %get-tuple-element.26), kind=kCustom, calls=%fused_computation.1 | custom fusion | bytes 4720896 | tf_op jit(solution)/shard_map/gather | solution.py:66
  43.3 5.0 %broadcast_multiply_fusion.1 = (bf16[4,144,2048]{2,1,0:T(8,128)(2,1)}, bf16[4,144,2048]{2,1,0:T(8,128)(2,1)}) fusion(bf16[4,144,2048]{2,1,0:T(8,128)(2,1)} %bitcast.58, bf16[4,144]{1,0:T(4,128)(2,1)S(1)} %mul.96, bf16[4,144,2048]{2,1,0:T(8,128)(2,1)} %bitcast.57), kind=kLoop, calls=%fused_computation.29 | loop fusion | flops 2359296 | bytes 9438336 | tf_op jit(solution)/shard_map/mul | solution.py:66
  48.3 33.0 %all_to_all.31 = bf16[4,144,2048]{2,1,0:T(8,128)(2,1)} all-to-all(bf16[4,144,2048]{2,1,0:T(8,128)(2,1)} %get-tuple-element.25), channel_id=1, replica_groups=mesh['rep'=8,'ep'=4] {'ep'}, dimensions={0} | all-to-all | bytes 4718592 | tf_op jit(solution)/shard_map/all_to_all | solution.py:69
  81.3 4.5 all-to-all-start.1
  85.8 0.2 reduce-scatter.5.cloned.1.call-start
  86.1 5.1 %fusion.2 = f32[576,768]{1,0:T(8,128)} fusion(bf16[576,2048]{1,0:T(8,128)(2,1)} %bitcast.59, bf16[1,2048,768]{2,1,0:T(8,128)(2,1)S(1)} %copy-done), kind=kOutput, calls=%fused_computation.10 | convolution fusion | flops 1811939328 | bytes 7274496 | tf_op jit(solution)/shard_map/dot_general | solution.py:30
  91.2 3.3 fusion.6
  94.5 19.8 %all-to-all-done.1 = bf16[4,144,2048]{2,1,0:T(8,128)(2,1)} async-done(((bf16[4,144,2048]{2,1,0:T(8,128)(2,1)}), bf16[4,144,2048]{2,1,0:T(8,128)(2,1)}, u32[]{:S(2)}, u32[]{:S(2)}) %all-to-all-start.1) | async-done | bytes 2359328 | tf_op jit(solution)/shard_map/all_to_all | solution.py:70
  114.3 8.1 %fusion.17 = f32[768,2048]{1,0:T(8,128)} fusion(bf16[576,2048]{1,0:T(8,128)(2,1)} %bitcast.2, f32[576]{0:T(1024)S(1)} %reshape.132, f32[576,768]{1,0:T(8,128)} %fusion.6, f32[576,768]{1,0:T(8,128)} %fusion.2), kind=kOutput, calls=%fused_computation.30 | convolution fusion | flops 1815035904 | bytes 12192000 | tf_op jit(solution)/shard_map/dot_general | solution.py:111
  122.5 6.5 %multiply_reduce_fusion = (bf16[576]{0:T(1024)(128)(2,1)S(1)}, bf16[576,768]{1,0:T(8,128)(2,1)S(1)}, bf16[576,768]{1,0:T(8,128)(2,1)S(1)}) fusion(f32[576,768]{1,0:T(8,128)} %fusion.6, f32[576,768]{1,0:T(8,128)} %fusion.2, f32[576]{0:T(1024)S(1)} %reshape.132, bf16[576,2048]{1,0:T(8,128)(2,1)} %bitcast.2, bf16[1,768,2048]{2,1,0:T(8,128)(2,1)} %param.13), kind=kOutput, calls=%fused_computation.23 | convolution fusion | flops 1819459072 | bytes 10816896 | tf_op jit(solution)/shard_map/dot_general | solution.py:35
  129.1 0.9 copy-done.5
  130.0 0.3 copy-done.6
  130.3 8.3 %fusion.12 = f32[2048,1536]{1,0:T(8,128)} fusion(bf16[576,2048]{1,0:T(8,128)(2,1)S(1)} %bitcast.61, bf16[576,768]{1,0:T(8,128)(2,1)S(1)} %get-tuple-element.19, bf16[576,768]{1,0:T(8,128)(2,1)S(1)} %get-tuple-element.18), kind=kOutput, calls=%fused_computation.18 | convolution fusion | flops 3627417600 | bytes 16711680 | tf_op jit(solution)/shard_map/dot_general | solution.py:102
  138.6 0.7 convert_element_type.60
  139.3 3.5 all-to-all-start.4
  142.8 3.4 fusion
  146.2 3.5 add_convert_fusion
  149.7 4.5 all-to-all-start.3
  154.2 0.1 reshape.130
  154.3 2.8 gather_fusion.4
  157.1 0.2 reshape.131
  157.3 0.7 copy.23
  157.9 24.8 %all-to-all-done.3 = bf16[4,144,2048]{2,1,0:T(8,128)(2,1)} async-done(((bf16[4,144,2048]{2,1,0:T(8,128)(2,1)}), bf16[4,144,2048]{2,1,0:T(8,128)(2,1)}, u32[]{:S(2)}, u32[]{:S(2)}) %all-to-all-start.3) | async-done | bytes 2359328 | tf_op jit(solution)/shard_map/all_to_all | solution.py:81
  182.7 7.1 %gather_fusion.3 = bf16[384,2048]{1,0:T(8,128)(2,1)} fusion(bf16[576,2048]{1,0:T(8,128)(2,1)} %bitcast.9, s32[1024]{0:T(1024)S(1)} %pad_clamp_fusion), kind=kCustom, calls=%fused_computation.3 | custom fusion | bytes 3147264 | tf_op jit(solution)/shard_map/gather | solution.py:92
  189.9 3.7 reshape.129
  193.6 6.2 %reduce_sum.34 = bf16[192,2048]{1,0:T(8,128)(2,1)} reduce(bf16[192,2,2048]{2,1,0:T(2,128)(2,1)} %reshape.129, bf16[]{:T(256)} %constant.36.clone.1), dimensions={1}, to_apply=%region_5.6 | reduce | flops 393216 | bytes 2359298 | tf_op jit(solution)/shard_map/reduce_sum | solution.py:93
  199.8 42.0 %reduce-scatter.5.cloned.1.call-done = f32[768,256]{1,0:T(8,128)} async-done(((f32[768,2048]{1,0:T(8,128)}), f32[768,256]{1,0:T(8,128)}) %reduce-scatter.5.cloned.1.call-update) | async-done | bytes 786448 | tf_op jit(solution)/shard_map/reduce_scatter | solution.py:112
  241.8 2.1 multiply_bitcast_fusion
  243.9 208.2 %reduce-scatter.3.cloned.1.call-done = f32[256,1536]{1,0:T(8,128)} async-done(((f32[2048,1536]{1,0:T(8,128)}), f32[256,1536]{1,0:T(8,128)}) %reduce-scatter.3.cloned.1.call-update) | async-done | bytes 1572880 | tf_op jit(solution)/shard_map/reduce_scatter | solution.py:101
  452.1 1.5 broadcast_multiply_fusion.2
  453.6 1.3 slice_bitcast_fusion
  (33 shorter events, 0.5 us)
Async XLA Ops:
  7.2 79.0 %copy-start = (bf16[1,2048,768]{2,1,0:T(8,128)(2,1)S(1)}, bf16[1,2048,768]{2,1,0:T(8,128)(2,1)}, u32[]{:S(2)}) copy-start(bf16[1,2048,768]{2,1,0:T(8,128)(2,1)} %param.11) | copy-start | bytes 9437188
  22.8 25.5 %all-to-all-start = ((bf16[4,1,144]{2,1,0:T(2,128)(2,1)}), bf16[4,1,144]{2,1,0:T(2,128)(2,1)S(1)}, u32[]{:S(2)}, u32[]{:S(2)}) async-start(bf16[4,1,144]{2,1,0:T(2,128)(2,1)} %all_to_all.25), calls=%async_computation | async-start | bytes 8192 | tf_op jit(solution)/shard_map/all_to_all | solution.py:71
  81.3 33.1 %all-to-all-start.1 = ((bf16[4,144,2048]{2,1,0:T(8,128)(2,1)}), bf16[4,144,2048]{2,1,0:T(8,128)(2,1)}, u32[]{:S(2)}, u32[]{:S(2)}) async-start(bf16[4,144,2048]{2,1,0:T(8,128)(2,1)} %get-tuple-element.24), calls=%async_computation.1 | async-start | bytes 4718592 | tf_op jit(solution)/shard_map/all_to_all | solution.py:70
  85.8 156.0 %reduce-scatter.5.cloned.1.call-start = ((), (), s32[]{:S(2)}) async-start(), calls=%async_computation.8 | async-start | bytes 7077888 | tf_op jit(solution)/shard_map/reduce_scatter | solution.py:112
  86.1 5.1 %copy-start.1 = (bf16[4,144,2048]{2,1,0:T(8,128)(2,1)S(1)}, bf16[4,144,2048]{2,1,0:T(8,128)(2,1)}, u32[]{:S(2)}) copy-start(bf16[4,144,2048]{2,1,0:T(8,128)(2,1)} %all_to_all.31) | copy-start | bytes 7077892
  86.1 5.1 %copy-start.3 = (bf16[1,2048,768]{2,1,0:T(8,128)(2,1)S(1)}, bf16[1,2048,768]{2,1,0:T(8,128)(2,1)}, u32[]{:S(2)}) copy-start(bf16[1,2048,768]{2,1,0:T(8,128)(2,1)} %param.12) | copy-start | bytes 9437188
  122.5 329.6 %reduce-scatter.3.cloned.1.call-start = ((), (), s32[]{:S(2)}) async-start(), calls=%async_computation.7 | async-start | bytes 14155776 | tf_op jit(solution)/shard_map/reduce_scatter | solution.py:101
  122.5 7.8 %copy-start.2 = (bf16[4,144,2048]{2,1,0:T(8,128)(2,1)S(1)}, bf16[4,144,2048]{2,1,0:T(8,128)(2,1)}, u32[]{:S(2)}) copy-start(bf16[4,144,2048]{2,1,0:T(8,128)(2,1)} %all_to_all.31) | copy-start | bytes 7077892
  129.0 0.9 copy-start.5
  129.0 1.2 copy-start.6
  139.3 10.4 %all-to-all-start.4 = ((bf16[4,1,144]{2,1,0:T(2,128)(2,1)}), bf16[4,1,144]{2,1,0:T(2,128)(2,1)S(1)}, u32[]{:S(2)}, u32[]{:S(2)}) async-start(bf16[4,1,144]{2,1,0:T(2,128)(2,1)} %convert_element_type.60), calls=%async_computation.4 | async-start | bytes 8192 | tf_op jit(solution)/shard_map/all_to_all | solution.py:88
  142.8 3.4 copy-start.4
  142.8 3.4 copy-start.7
  149.7 33.0 %all-to-all-start.3 = ((bf16[4,144,2048]{2,1,0:T(8,128)(2,1)}), bf16[4,144,2048]{2,1,0:T(8,128)(2,1)}, u32[]{:S(2)}, u32[]{:S(2)}) async-start(bf16[4,144,2048]{2,1,0:T(8,128)(2,1)} %bitcast.62), calls=%async_computation.3 | async-start | bytes 4718592 | tf_op jit(solution)/shard_map/all_to_all | solution.py:81
Sparse Core Ops, SparseCore 0:
  122.6 119.1 reduce-scatter.4
  245.4 206.6 reduce-scatter.2
where the time goes:
time: 462 us
  waiting for transfers between devices  295 us (64%)
  local copies, waits for them, and re-layouts  47.3 us (10%)
  matrix products  38.1 us (8%)
  blocking collectives  33 us (7%)
  other arithmetic  17.1 us (4%)
  starting transfers between devices  17 us (4%)
  between operations  14.3 us (3%)
    reduce_scatter x1, waiting for transfers between devices, body(): lax.psum_scatter(lax.dot_general(expert_in, pair_grad, contract, preferre...  208 us
    reduce_scatter x1, waiting for transfers between devices, body(): lax.psum_scatter(down_term, 'rep', scatter_dimension=1, tiled=True)  42 us
    all_to_all x1, blocking collectives, body(): lax.all_to_all(send_in, 'ep', split_axis=0, concat_axis=0, tiled=True)  33 us
    all_to_all x1, waiting for transfers between devices, body(): lax.all_to_all(routed.reshape(ep_count, capacity, model_width), 'ep', spl...  24.8 us
    all_to_all x1, waiting for transfers between devices, body(): lax.all_to_all(send_up, 'ep', split_axis=0, concat_axis=0, tiled=True)  19.8 us
  transfers between devices with their start and end apart: 6, of which 4 were waited for; matrix products, arithmetic and copies ran while one was open for 16% of the time, Pallas kernels for 0%

commit v1 on v0

v1 whole, which is shorter than its diff:
```python
import jax
import jax.numpy as jnp
from jax import lax
from jax.experimental import pallas as pl
from jax.experimental.pallas import tpu as pltpu
from jax.sharding import PartitionSpec as P


F32 = jnp.float32
BF16 = jnp.bfloat16
ROWS = (((0,), (0,)), ((), ()))
COLS = (((1,), (1,)), ((), ()))


def swap(value, axis, mask):
    count = lax.axis_size(axis)
    return lax.ppermute(value, axis, [(i, i ^ mask) for i in range(count)])


def after(value, *earlier):
    return lax.optimization_barrier((value,) + earlier)[0]


def lane_block(size, most=256):
    return most if size % most == 0 else size


def pick_columns(scalars, offset, count, value, width):
    rows = value.shape[0]

    def kernel(scalar_ref, in_ref, out_ref):
        for k in range(count):
            start = pl.multiple_of(scalar_ref[offset + k] * width, width)
            out_ref[:, k * width : (k + 1) * width] = in_ref[:, pl.ds(start, width)]

    return pl.pallas_call(
        kernel,
        grid_spec=pltpu.PrefetchScalarGridSpec(
            num_scalar_prefetch=1,
            grid=(1,),
            in_specs=[pl.BlockSpec(value.shape, lambda k, t: (0, 0))],
            out_specs=pl.BlockSpec((rows, count * width), lambda k, t: (0, 0)),
        ),
        out_shape=jax.ShapeDtypeStruct((rows, count * width), value.dtype),
    )(scalars, value)


def prob_of(coef_refs, expert):
    parts = []
    for ref in coef_refs:
        lanes = lax.broadcasted_iota(jnp.int32, ref.shape, 1)
        parts.append(jnp.where(lanes == expert, ref[...].astype(F32), 0.0))
    return jnp.sum(jnp.concatenate(parts, axis=0), axis=1, keepdims=True)


def activations(expert, coefs, tokens, gate_w, up_w):
    rows, width = tokens[0].shape
    hidden = gate_w.shape[1]
    total = rows * len(tokens)
    block = lane_block(hidden)
    count = len(tokens)

    def kernel(expert_ref, *refs):
        coef_refs, token_refs = refs[:count], refs[count : 2 * count]
        gate_ref, up_ref, gate_out, up_out, weighted_out, rows_ref = refs[2 * count :]

        @pl.when(pl.program_id(0) == 0)
        def _():
            for j, ref in enumerate(token_refs):
                rows_ref[j * rows : (j + 1) * rows, :] = ref[...]

        x = rows_ref[...]
        gate = jnp.dot(x, gate_ref[...], preferred_element_type=F32)
        up = jnp.dot(x, up_ref[...], preferred_element_type=F32)
        gate_out[...] = gate
        up_out[...] = up
        activation = gate * jax.nn.sigmoid(gate) * up
        weighted_out[...] = (prob_of(coef_refs, expert_ref[0]) * activation).astype(BF16)

    whole = [pl.BlockSpec(c.shape, lambda k, e: (0, 0)) for c in coefs]
    whole += [pl.BlockSpec(t.shape, lambda k, e: (0, 0)) for t in tokens]
    column = pl.BlockSpec((width, block), lambda k, e: (0, k))
    out = pl.BlockSpec((total, block), lambda k, e: (0, k))
    return pl.pallas_call(
        kernel,
        grid_spec=pltpu.PrefetchScalarGridSpec(
            num_scalar_prefetch=1,
            grid=(hidden // block,),
            in_specs=whole + [column, column],
            out_specs=[out, out, out],
            scratch_shapes=[pltpu.VMEM((total, width), BF16)],
        ),
        out_shape=[
            jax.ShapeDtypeStruct((total, hidden), F32),
            jax.ShapeDtypeStruct((total, hidden), F32),
            jax.ShapeDtypeStruct((total, hidden), BF16),
        ],
        cost_estimate=pl.CostEstimate(
            flops=4 * total * width * hidden, bytes_accessed=4 * width * hidden, transcendentals=0
        ),
    )(expert, *coefs, *tokens, gate_w, up_w)


def hidden_grads(scalars, coefs, parts, down_w, gate_act, up_act, own_width):
    rows = parts[0][0].shape[0]
    hidden, width = down_w.shape
    total = rows * len(parts)
    block = lane_block(hidden)
    count = len(parts)
    flat = [part for pair in parts for part in pair]
    per_row = len(parts[0])

    def kernel(scalar_ref, *refs):
        coef_refs, part_refs = refs[:count], refs[count : count + len(flat)]
        down_ref, gate_ref, up_ref, gate_out, up_out, prob_out, rows_ref, sum_ref = refs[count + len(flat) :]
        step = pl.program_id(0)

        @pl.when(step == 0)
        def _():
            for i, ref in enumerate(part_refs):
                j, h = divmod(i, per_row)
                blocks = ref.shape[1] // own_width
                for b in range(blocks):
                    owner = scalar_ref[1 + h * blocks + b]
                    start = pl.multiple_of(owner * own_width, own_width)
                    rows_ref[j * rows : (j + 1) * rows, pl.ds(start, own_width)] = ref[
                        :, b * own_width : (b + 1) * own_width
                    ]
            sum_ref[...] = jnp.zeros_like(sum_ref)

        back = lax.dot_general(rows_ref[...], down_ref[...], COLS, preferred_element_type=F32)
        gate, up = gate_ref[...], up_ref[...]
        s = jax.nn.sigmoid(gate)
        silu = gate * s
        sum_ref[...] += jnp.sum(silu * up * back, axis=1, keepdims=True)
        act_grad = prob_of(coef_refs, scalar_ref[0]) * back
        gate_out[...] = (act_grad * up * s * (1.0 + gate * (1.0 - s))).astype(BF16)
        up_out[...] = (act_grad * silu).astype(BF16)

        @pl.when(step == pl.num_programs(0) - 1)
        def _():
            prob_out[...] = sum_ref[...].astype(BF16)

    whole = [pl.BlockSpec(c.shape, lambda k, e: (0, 0)) for c in coefs]
    whole += [pl.BlockSpec(t.shape, lambda k, e: (0, 0)) for t in flat]
    column = pl.BlockSpec((total, block), lambda k, e: (0, k))
    return pl.pallas_call(
        kernel,
        grid_spec=pltpu.PrefetchScalarGridSpec(
            num_scalar_prefetch=1,
            grid=(hidden // block,),
            in_specs=whole + [pl.BlockSpec((block, width), lambda k, e: (k, 0)), column, column],
            out_specs=[column, column, pl.BlockSpec((total, 1), lambda k, e: (0, 0))],
            scratch_shapes=[pltpu.VMEM((total, width), BF16), pltpu.VMEM((total, 1), F32)],
        ),
        out_shape=[
            jax.ShapeDtypeStruct((total, hidden), BF16),
            jax.ShapeDtypeStruct((total, hidden), BF16),
            jax.ShapeDtypeStruct((total, 1), BF16),
        ],
        cost_estimate=pl.CostEstimate(
            flops=2 * total * width * hidden, bytes_accessed=2 * width * hidden, transcendentals=0
        ),
    )(scalars, *coefs, *flat, down_w, gate_act, up_act)


def weight_blocks(scalars, offset, count, rows, grads, own_width, flip, dtype):
    per_group = len(rows) // len(grads)
    hidden = grads[0].shape[1]
    tok_rows = rows[0].shape[0]
    shape = (hidden, own_width) if flip else (own_width, hidden)

    def kernel(scalar_ref, *refs):
        row_refs, grad_refs, out_ref = refs[: len(rows)], refs[len(rows) : -1], refs[-1]
        where = scalar_ref[offset + pl.program_id(0)] if offset is not None else pl.program_id(0)
        lanes = pl.ds(pl.multiple_of(where * own_width, own_width), own_width)
        acc = None
        for g, grad_ref in enumerate(grad_refs):
            x = jnp.concatenate([r[:, lanes] for r in row_refs[g * per_group : (g + 1) * per_group]], axis=0)
            pair = (grad_ref[...], x) if flip else (x, grad_ref[...])
            term = lax.dot_general(*pair, ROWS, preferred_element_type=F32)
            acc = term if acc is None else acc + term
        out_ref[0] = acc.astype(dtype)

    in_specs = [pl.BlockSpec(x.shape, lambda k, t: (0, 0)) for x in list(rows) + list(grads)]
    return pl.pallas_call(
        kernel,
        grid_spec=pltpu.PrefetchScalarGridSpec(
            num_scalar_prefetch=1,
            grid=(count,),
            in_specs=in_specs,
            out_specs=pl.BlockSpec((1,) + shape, lambda k, t: (k, 0, 0)),
        ),
        out_shape=jax.ShapeDtypeStruct((count,) + shape, dtype),
        cost_estimate=pl.CostEstimate(
            flops=2 * count * own_width * hidden * tok_rows * len(rows),
            bytes_accessed=2 * count * own_width * tok_rows * len(rows),
            transcendentals=0,
        ),
    )(scalars, *rows, *grads)


def masks_of(bits):
    masks = [0]
    for bit in reversed(bits):
        masks = [bit | m for m in masks] + masks
    return masks


def step(tokens, upstream, route_ids, route_probs, gate_proj, up_proj, down_proj):
    ep_count = lax.axis_size("ep")
    rep_count = lax.axis_size("rep")
    ep_index = lax.axis_index("ep")
    rep_index = lax.axis_index("rep")
    tok_rows, model_width = tokens.shape
    own_width = model_width // rep_count
    half = rep_count // 2
    gate_w, up_w, down_w = gate_proj[0], up_proj[0], down_proj[0]
    bits = [1 << i for i in range(rep_count.bit_length() - 1)]
    turned = [bits[1], bits[0]] + bits[2:]
    near_masks, turned_masks = masks_of(bits[1:]), masks_of(turned[1:])
    far_masks, turned_far_masks = [bits[0] | m for m in near_masks], [turned[0] | m for m in turned_masks]
    chip_masks = list(range(0, ep_count, 2))

    lists = far_masks + near_masks + turned_far_masks + turned_masks
    scalars = jnp.concatenate(
        [ep_index.reshape(1).astype(jnp.int32), rep_index ^ jnp.array(lists, jnp.int32)]
    )
    far_at, near_at, turned_far_at, turned_at = (1 + i * half for i in range(4))

    def across(value):
        blocks = {}
        for mask in chip_masks[1:]:
            blocks[mask] = swap(value, "ep", mask)
        blocks[0], blocks[1] = value, swap(value, "ep", 1)
        return blocks

    def forward(blocks, *earlier):
        for mask in chip_masks[1:]:
            blocks[mask] = after(blocks[mask], *earlier)
            blocks[mask | 1] = swap(blocks[mask], "ep", 1)

    token_rows = across(tokens)
    up_far = across(pick_columns(scalars, far_at, half, upstream, own_width))
    up_near = across(pick_columns(scalars, near_at, half, upstream, own_width))
    lanes = jnp.arange(ep_count, dtype=jnp.int32)
    coef = jnp.sum(
        jnp.where(route_ids[:, :, None] == lanes[None, None, :], route_probs[:, :, None].astype(F32), 0.0),
        axis=1,
    ).astype(BF16)
    coefs = {j: swap(coef, "ep", j) if j else coef for j in range(ep_count)}

    acts, grads = {}, {}

    def act(mask, *earlier):
        pair = (mask, mask | 1)
        rows = [token_rows[j] for j in pair]
        rows[0] = after(rows[0], *earlier)
        acts[mask] = activations(scalars, [coefs[j] for j in pair], rows, gate_w, up_w)

    def hidden(mask, *earlier):
        pair = (mask, mask | 1)
        parts = [(up_far[j], up_near[j]) for j in pair]
        grads[mask] = hidden_grads(
            scalars, [coefs[j] for j in pair], parts, down_w, after(acts[mask][0], *earlier), acts[mask][1], own_width
        )

    act(0)
    forward(token_rows, acts[0][0])
    hidden(0)
    forward(up_far, grads[0][0])
    for mask in chip_masks[1:]:
        act(mask, grads[0][0])
    forward(up_near, acts[chip_masks[-1]][0])
    up_far_list = [up_far[j] for j in range(ep_count)]
    token_list = [token_rows[j] for j in range(ep_count)]
    weighted = [acts[mask][2] for mask in chip_masks]

    def outer(offset, rows, grad, flip, dtype):
        return weight_blocks(scalars, offset, half, rows, grad, own_width, flip, dtype)

    down_send = outer(None, up_far_list, weighted, True, BF16)
    down_got = swap(down_send, "rep", bits[0])
    for mask in chip_masks[1:]:
        hidden(mask, down_send)
    up_near_list = [up_near[j] for j in range(ep_count)]
    gate_grads = [grads[mask][0] for mask in chip_masks]
    up_grads = [grads[mask][1] for mask in chip_masks]
    up_send = outer(turned_far_at, token_list, up_grads, False, BF16)
    up_got = swap(up_send, "rep", turned[0])
    gate_grads[0] = after(gate_grads[0], up_send)
    gate_send = outer(far_at, token_list, gate_grads, False, BF16)
    gate_got = swap(gate_send, "rep", bits[0])

    routed = {}
    for mask, gate_grad, up_grad in reversed(list(zip(chip_masks, gate_grads, up_grads))):
        gate_grad = after(gate_grad, gate_send)
        both = lax.dot_general(gate_grad, gate_w, COLS, preferred_element_type=F32)
        both = both + lax.dot_general(up_grad, up_w, COLS, preferred_element_type=F32)
        both = both.astype(BF16)
        routed[mask], routed[mask | 1] = both[:tok_rows], both[tok_rows:]
    back = {mask: swap(routed[mask | 1], "ep", 1) for mask in chip_masks}
    down_keep = outer(None, up_near_list, [after(weighted[0], routed[0])] + weighted[1:], True, F32)
    up_keep = outer(turned_at, token_list, [after(up_grads[0], down_keep)] + up_grads[1:], False, F32)
    sums = {mask: routed[mask].astype(F32) + back[mask].astype(F32) for mask in chip_masks}
    far_sums = [swap(sums[mask].astype(BF16), "ep", mask) for mask in chip_masks[1:]]
    gate_keep = outer(near_at, token_list, [after(gate_grads[0], up_keep)] + gate_grads[1:], False, F32)
    probs_back = []
    for j in range(1, ep_count):
        block = grads[j & ~1][2][(j & 1) * tok_rows : (1 + (j & 1)) * tok_rows]
        probs_back.append(swap(block, "ep", j))

    state = {
        "down": [down_got, down_keep, bits, 0],
        "up": [up_got, up_keep, turned, 0],
        "gate": [gate_got, gate_keep, bits, 0],
    }
    done = [gate_keep]

    def advance(name):
        got, keep, order, at = state[name]
        got = after(got, done[0])
        keep = keep + got.astype(F32)
        if at + 1 == len(order):
            state[name] = keep * (1.0 / rep_count)
            return
        middle = keep.shape[0] // 2
        send = keep[:middle].astype(BF16)
        done[0] = send
        got = swap(send, "rep", order[at + 1])
        state[name] = [got, keep[middle:], order, at + 1]

    advance("down")
    advance("up")
    far_sums = [after(value, done[0]) for value in far_sums]
    token_sum = sums[0]
    for value in far_sums:
        token_sum = token_sum + value.astype(F32)
    grad_tokens = token_sum.astype(BF16)
    own_probs = grads[0][2][:tok_rows]
    grad_probs = 0.0
    for j, block in enumerate([own_probs] + [after(p, done[0]) for p in probs_back]):
        grad_probs = grad_probs + jnp.where(route_ids == ep_index ^ j, block.astype(F32), 0.0)
    levels = range(len(bits))
    events = [(level, 0, "down") for level in levels] + [(level + 1, 2, "gate") for level in levels]
    events += [(level + (level > 0), 1, "up") for level in levels]
    for _, _, name in sorted(events)[2:]:
        advance(name)
    return (grad_tokens, grad_probs.astype(BF16), state["gate"], state["up"], state["down"])


def solution(mesh):
    return jax.shard_map(
        step,
        mesh=mesh,
        in_specs=(
            P(("rep", "ep"), None),
            P(("rep", "ep"), None),
            P(("rep", "ep"), None),
            P(("rep", "ep"), None),
            P("ep", None, None),
            P("ep", None, None),
            P("ep", None, None),
        ),
        out_specs=(
            P(("rep", "ep"), None),
            P(("rep", "ep"), None),
            P("ep", "rep", None),
            P("ep", "rep", None),
            P("ep", None, "rep"),
        ),
        check_vma=False,
    )
```

time: 462 us -> 216 us (0.47)
  waiting for transfers between devices: 295 us -> 81.3 us
  Pallas kernels: 0 us -> 72.5 us
  local copies, waits for them, and re-layouts: 47.3 us -> 6.88 us
  blocking collectives: 33 us -> 0 us
  matrix products: 38.1 us -> 14.1 us
  between operations: 14.3 us -> 0.99 us
  starting transfers between devices: 17 us -> 24.9 us
    reduce_scatter x2 -> x0, waiting for transfers between devices: 250 us -> none  [the longest x1 208 us: body(): lax.psum_scatter(lax.dot_general(expert_in, pair_grad, contract, preferre...]
    ppermute x0 -> x27, waiting for transfers between devices: none -> 81.3 us  [swap(): return lax.ppermute(value, axis, [(i, i ^ mask) for i in range(count)])]
    pallas_call x0 -> x12, Pallas kernels: none -> 72.5 us  [the longest x6 37.8 us: weight_blocks(): pl.pallas_call(kernel, grid_spec=pltpu.PrefetchScalarGridSpec(num_scalar_...]
    all_to_all x4 -> x0, waiting for transfers between devices: 44.6 us -> none  [the longest x1 24.8 us: body(): lax.all_to_all(routed.reshape(ep_count, capacity, model_width), 'ep', spl...]
    all_to_all x1 -> x0, blocking collectives: 33 us -> none  [body(): lax.all_to_all(send_in, 'ep', split_axis=0, concat_axis=0, tiled=True)]
    gather x5 -> x0, local copies, waits for them, and re-layouts: 30.1 us -> none  [the longest x1 8.08 us: body(): tokens[owner_row] * keep_mask[:, None]]
    ppermute x0 -> x27, starting transfers between devices: none -> 24.9 us  [swap(): return lax.ppermute(value, axis, [(i, i ^ mask) for i in range(count)])]
    dot_general x7 -> x4, matrix products: 38.1 us -> 14.1 us  [the longest x2 8.23 us: step(): lax.dot_general(up_grad, up_w, COLS, preferred_element_type=F32)]
  transfers between devices with their start and end apart: 6 -> 27, of which waited for: 4 -> 12; matrix products, arithmetic and copies ran while one was open for 16% -> 13% of each run, Pallas kernels for 0% -> 34%
where the time goes in v1:
time: 216 us; the launch traced here: 215 us
  waiting for transfers between devices  81.3 us (38%)
  Pallas kernels  72.5 us (34%)
  starting transfers between devices  24.9 us (12%)
  other arithmetic  14.7 us (7%)
  matrix products  14.1 us (7%)
  local copies, waits for them, and re-layouts  6.88 us (3%)
    ppermute x27, waiting for transfers between devices, swap(): return lax.ppermute(value, axis, [(i, i ^ mask) for i in range(count)])  81.3 us
    pallas_call x6, Pallas kernels, weight_blocks(): pl.pallas_call(kernel, grid_spec=pltpu.PrefetchScalarGridSpec(num_scalar_...  37.8 us
    ppermute x27, starting transfers between devices, swap(): return lax.ppermute(value, axis, [(i, i ^ mask) for i in range(count)])  24.9 us
    pallas_call x2, Pallas kernels, activations(): pl.pallas_call(kernel, grid_spec=pltpu.PrefetchScalarGridSpec(num_scalar_...  15.5 us
    pallas_call x2, Pallas kernels, hidden_grads(): pl.pallas_call(kernel, grid_spec=pltpu.PrefetchScalarGridSpec(num_scalar_...  13.9 us
    dot_general x2, matrix products, step(): lax.dot_general(up_grad, up_w, COLS, preferred_element_type=F32)  8.23 us
    add x6, other arithmetic, advance(): keep = keep + got.astype(F32)  6 us
    dot_general x2, matrix products, step(): both = lax.dot_general(gate_grad, gate_w, COLS, preferred_element_type=F32)  5.83 us
  transfers between devices with their start and end apart: 27, of which 12 were waited for; matrix products, arithmetic and copies ran while one was open for 13% of the time, Pallas kernels for 34%

profile of v1, /device:TPU:0, one launch (start us, length us, event | category | flops | bytes accessed | tf_op | source)
XLA Modules:
  0.0 215.4 jit_solution(11822419250969863318)
XLA Ops:
  1.2 2.6 %collective-permute-start.4 = (bf16[192,2048]{1,0:T(8,128)(2,1)}, bf16[192,2048]{1,0:T(8,128)(2,1)S(1)}, u32[]{:S(2)}, u32[]{:S(2)}) collective-permute-start(bf16[192,2048]{1,0:T(8,128)(2,1)} %refs_0_.7), channel_id=1, source_target_pairs={{0,2},{1,3},{2,0},{3,1},{4,6},{5,7},{6,4},{7,5},{8,10},{9,11},{10,... | collective-permute-start | bytes 2359304 | tf_op jit(solution)/shard_map/ppermute | solution.py:17
  7.7 7.8 %shard_map.121 = (f32[384,768]{1,0:T(8,128)}, f32[384,768]{1,0:T(8,128)}, bf16[384,768]{1,0:T(8,128)(2,1)}) custom-call(s32[17]{0:T(128)} %pad_add_fusion.scalar_ref.expert_ref, bf16[192,4]{1,0:T(8,128)(2,1)} %copy-done.16, bf16[192,4]{1,0:T(8,128)(2,1)} %copy-done.19, bf16[192,2048]{1,0:T(8,128)(2,1)} %refs_0_.7, bf16[192,2048]{1,0:T(8,128)(2,1)} %copy-done.3, ...), custom_call_target="tpu_custom_call" | custom-call | flops 2415919104 | bytes 6291456 | tf_op jit(solution)/shard_map/pallas_call | solution.py:84
  15.5 6.7 %collective-permute-done.4.refs_2_ = bf16[192,2048]{1,0:T(8,128)(2,1)S(1)} collective-permute-done((bf16[192,2048]{1,0:T(8,128)(2,1)}, bf16[192,2048]{1,0:T(8,128)(2,1)S(1)}, u32[]{:S(2)}, u32[]{:S(2)}) %collective-permute-start.4) | collective-permute-done | bytes 786464 | tf_op jit(solution)/shard_map/ppermute | solution.py:17
  22.1 2.6 %shard_map.119.refs_2_.refs_0_ = bf16[192,1024]{1,0:T(8,128)(2,1)} custom-call(s32[17]{0:T(128)} %pad_add_fusion.scalar_ref.expert_ref, bf16[192,2048]{1,0:T(8,128)(2,1)} %in_ref.3), custom_call_target="tpu_custom_call" | custom-call | tf_op jit(solution)/shard_map/pallas_call | solution.py:36
  25.2 2.6 %shard_map.120.refs_3_.refs_0_ = bf16[192,1024]{1,0:T(8,128)(2,1)} custom-call(s32[17]{0:T(128)} %pad_add_fusion.scalar_ref.expert_ref, bf16[192,2048]{1,0:T(8,128)(2,1)} %in_ref.3), custom_call_target="tpu_custom_call" | custom-call | tf_op jit(solution)/shard_map/pallas_call | solution.py:36
  27.8 1.7 collective-permute-start.8
  29.9 1.7 collective-permute-start.6
  31.6 0.8 copy-done.9
  32.4 7.0 %shard_map.122 = (bf16[384,768]{1,0:T(8,128)(2,1)}, bf16[384,768]{1,0:T(8,128)(2,1)}, bf16[384,1]{1,0:T(8,128)(2,1)}) custom-call(s32[17]{0:T(128)} %pad_add_fusion.scalar_ref.expert_ref, bf16[192,4]{1,0:T(8,128)(2,1)} %copy-done.16, bf16[192,4]{1,0:T(8,128)(2,1)} %copy-done.19, bf16[192,1024]{1,0:T(8,128)(2,1)} %shard_map.119.refs_2_.refs_0_, ...), custom_call_target="tpu_custom_call" | custom-call | flops 1207959552 | bytes 3145728 | tf_op jit(solution)/shard_map/pallas_call | solution.py:147
  40.0 9.5 %collective-permute-done.6.refs_0_ = bf16[192,4]{1,0:T(8,128)(2,1)S(1)} collective-permute-done((bf16[192,4]{1,0:T(8,128)(2,1)}, bf16[192,4]{1,0:T(8,128)(2,1)S(1)}, u32[]{:S(2)}, u32[]{:S(2)}) %collective-permute-start.6) | collective-permute-done | bytes 1568 | tf_op jit(solution)/shard_map/ppermute | solution.py:17
  50.3 0.9 copy-done.5
  51.1 7.8 %shard_map.123 = (f32[384,768]{1,0:T(8,128)}, f32[384,768]{1,0:T(8,128)}, bf16[384,768]{1,0:T(8,128)(2,1)}) custom-call(s32[17]{0:T(128)} %pad_add_fusion.scalar_ref.expert_ref, bf16[192,4]{1,0:T(8,128)(2,1)} %copy-done.20, bf16[192,4]{1,0:T(8,128)(2,1)} %copy-done.21, bf16[192,2048]{1,0:T(8,128)(2,1)} %copy-done.4, bf16[192,2048]{1,0:T(8,128)(2,1)} %copy-done.5, ...), custom_call_target="tpu_custom_call" | custom-call | flops 2415919104 | bytes 6291456 | tf_op jit(solution)/shard_map/pallas_call | solution.py:84
  59.3 0.8 copy-done.15
  60.1 5.8 %shard_map.124 = bf16[4,768,256]{2,1,0:T(8,128)(2,1)} custom-call(s32[17]{0:T(128)} %pad_add_fusion.scalar_ref.expert_ref, bf16[192,1024]{1,0:T(8,128)(2,1)} %shard_map.119.refs_2_.refs_0_, bf16[192,1024]{1,0:T(8,128)(2,1)} %copy-done.14, bf16[192,1024]{1,0:T(8,128)(2,1)} %copy-done.13, bf16[192,1024]{1,0:T(8,128)(2,1)} %copy-done.15, ...), custom_call_target="tpu_custom_call" | custom-call | flops 1207959552 | bytes 1572864 | tf_op jit(solution)/shard_map/pallas_call | solution.py:186
  65.8 1.7 collective-permute-start.16
  67.6 0.7 copy-done.11
  68.3 6.9 %shard_map.125 = (bf16[384,768]{1,0:T(8,128)(2,1)}, bf16[384,768]{1,0:T(8,128)(2,1)}, bf16[384,1]{1,0:T(8,128)(2,1)}) custom-call(s32[17]{0:T(128)} %pad_add_fusion.scalar_ref.expert_ref, bf16[192,4]{1,0:T(8,128)(2,1)} %copy-done.20, bf16[192,4]{1,0:T(8,128)(2,1)} %copy-done.21, bf16[192,1024]{1,0:T(8,128)(2,1)} %copy-done.13, bf16[192,1024]{1,0:T(8,128)(2,1)} %copy-done.10, ...), custom_call_target="tpu_custom_call" | custom-call | flops 1207959552 | bytes 3145728 | tf_op jit(solution)/shard_map/pallas_call | solution.py:147
  75.2 5.2 %fusion.7 = f32[384,2048]{1,0:T(8,128)} fusion(bf16[384,768]{1,0:T(8,128)(2,1)} %get-tuple-element.54.refs_5_, bf16[1,2048,768]{2,1,0:T(8,128)(2,1)} %param.13), kind=kOutput, calls=%fused_computation.38 | convolution fusion | flops 1207959552 | bytes 6881280 | tf_op jit(solution)/shard_map/dot_general | solution.py:299
  80.4 6.3 %shard_map.126 = bf16[4,256,768]{2,1,0:T(8,128)(2,1)} custom-call(s32[17]{0:T(128)} %pad_add_fusion.scalar_ref.expert_ref, bf16[192,2048]{1,0:T(8,128)(2,1)} %refs_0_.7, bf16[192,2048]{1,0:T(8,128)(2,1)} %copy-done.3, bf16[192,2048]{1,0:T(8,128)(2,1)} %copy-done.4, bf16[192,2048]{1,0:T(8,128)(2,1)} %copy-done.5, bf16[384,768]{1,0:T(8,128)(2,1)} %get-tuple-element.60.refs_4_, ...), custom_call_target="tpu_custom_call" | custom-call | flops 1207959552 | bytes 1572864 | tf_op jit(solution)/shard_map/pallas_call | solution.py:186
  86.6 6.4 %shard_map.127 = bf16[4,256,768]{2,1,0:T(8,128)(2,1)} custom-call(s32[17]{0:T(128)} %pad_add_fusion.scalar_ref.expert_ref, bf16[192,2048]{1,0:T(8,128)(2,1)} %refs_0_.7, bf16[192,2048]{1,0:T(8,128)(2,1)} %copy-done.3, bf16[192,2048]{1,0:T(8,128)(2,1)} %copy-done.4, bf16[192,2048]{1,0:T(8,128)(2,1)} %copy-done.5, bf16[384,768]{1,0:T(8,128)(2,1)} %get-tuple-element.57.refs_4_, ...), custom_call_target="tpu_custom_call" | custom-call | flops 1207959552 | bytes 1572864 | tf_op jit(solution)/shard_map/pallas_call | solution.py:186
  93.0 4.4 %add_convert_fusion = bf16[384,2048]{1,0:T(8,128)(2,1)S(1)} fusion(f32[384,2048]{1,0:T(8,128)} %fusion.7, bf16[384,768]{1,0:T(8,128)(2,1)S(1)} %copy-done.8, bf16[1,2048,768]{2,1,0:T(8,128)(2,1)} %param.12), kind=kOutput, calls=%fused_computation.3 | convolution fusion | flops 1209532416 | bytes 8454144 | tf_op jit(solution)/shard_map/dot_general | solution.py:298
  97.5 1.0 slice.89
  98.5 3.1 %fusion.9 = f32[384,2048]{1,0:T(8,128)} fusion(bf16[384,768]{1,0:T(8,128)(2,1)S(1)} %copy-done.7, bf16[1,2048,768]{2,1,0:T(8,128)(2,1)S(1)} %copy-done.23), kind=kOutput, calls=%fused_computation.40 | convolution fusion | flops 1207959552 | bytes 6881280 | tf_op jit(solution)/shard_map/dot_general | solution.py:299
  102.1 1.8 collective-permute-start.15
  103.9 1.6 collective-permute-start.18
  105.5 6.0 %shard_map.128 = f32[4,768,256]{2,1,0:T(8,128)} custom-call(s32[17]{0:T(128)} %pad_add_fusion.scalar_ref.expert_ref, bf16[192,1024]{1,0:T(8,128)(2,1)} %shard_map.120.refs_3_.refs_0_, bf16[192,1024]{1,0:T(8,128)(2,1)} %copy-done.9, bf16[192,1024]{1,0:T(8,128)(2,1)} %copy-done.10, bf16[192,1024]{1,0:T(8,128)(2,1)} %copy-done.11, ...), custom_call_target="tpu_custom_call" | custom-call | flops 1207959552 | bytes 1572864 | tf_op jit(solution)/shard_map/pallas_call | solution.py:186
  111.5 6.6 %shard_map.129 = f32[4,256,768]{2,1,0:T(8,128)} custom-call(s32[17]{0:T(128)} %pad_add_fusion.scalar_ref.expert_ref, bf16[192,2048]{1,0:T(8,128)(2,1)} %refs_0_.7, bf16[192,2048]{1,0:T(8,128)(2,1)} %copy-done.3, bf16[192,2048]{1,0:T(8,128)(2,1)} %copy-done.4, bf16[192,2048]{1,0:T(8,128)(2,1)} %copy-done.5, bf16[384,768]{1,0:T(8,128)(2,1)} %get-tuple-element.60.refs_4_, ...), custom_call_target="tpu_custom_call" | custom-call | flops 1207959552 | bytes 1572864 | tf_op jit(solution)/shard_map/pallas_call | solution.py:186
  118.1 6.8 %shard_map.130 = f32[4,256,768]{2,1,0:T(8,128)} custom-call(s32[17]{0:T(128)} %pad_add_fusion.scalar_ref.expert_ref, bf16[192,2048]{1,0:T(8,128)(2,1)} %refs_0_.7, bf16[192,2048]{1,0:T(8,128)(2,1)} %copy-done.3, bf16[192,2048]{1,0:T(8,128)(2,1)} %copy-done.4, bf16[192,2048]{1,0:T(8,128)(2,1)} %copy-done.5, bf16[384,768]{1,0:T(8,128)(2,1)} %get-tuple-element.57.refs_4_, ...), custom_call_target="tpu_custom_call" | custom-call | flops 1207959552 | bytes 1572864 | tf_op jit(solution)/shard_map/pallas_call | solution.py:186
  124.9 1.6 add_convert_fusion.3
  127.2 2.1 convert_add_fusion.2
  130.1 1.4 add_convert_fusion.1
  131.6 8.1 %collective-permute-done.15 = bf16[4,256,768]{2,1,0:T(8,128)(2,1)} collective-permute-done((bf16[4,256,768]{2,1,0:T(8,128)(2,1)}, bf16[4,256,768]{2,1,0:T(8,128)(2,1)}, u32[]{:S(2)}, u32[]{:S(2)}) %collective-permute-start.15) | collective-permute-done | bytes 1572896 | tf_op jit(solution)/shard_map/ppermute | solution.py:17
  139.7 1.7 convert_add_fusion.1
  141.4 4.1 %collective-permute-done.19 = bf16[192,1]{1,0:T(8,128)(2,1)S(1)} collective-permute-done((bf16[192,1]{1,0:T(8,128)(2,1)S(1)}, bf16[192,1]{1,0:T(8,128)(2,1)S(1)}, u32[]{:S(2)}, u32[]{:S(2)}) %collective-permute-start.19) | collective-permute-done | bytes 416 | tf_op jit(solution)/shard_map/ppermute | solution.py:17
  145.5 1.4 collective-permute-start.17
  147.8 1.5 collective-permute-start.23
  149.5 6.2 %collective-permute-done.21 = bf16[2,768,256]{2,1,0:T(8,128)(2,1)S(1)} collective-permute-done((bf16[2,768,256]{2,1,0:T(8,128)(2,1)S(1)}, bf16[2,768,256]{2,1,0:T(8,128)(2,1)S(1)}, u32[]{:S(2)}, u32[]{:S(2)}) %collective-permute-start.21) | collective-permute-done | bytes 786464 | tf_op jit(solution)/shard_map/ppermute | solution.py:17
  156.0 1.7 convert_add_fusion
  157.8 1.8 collective-permute-start.22
  159.6 1.3 add_convert_fusion.2
  160.9 2.6 %collective-permute-start.26 = (bf16[1,768,256]{2,1,0:T(8,128)(2,1)S(1)}, bf16[1,768,256]{2,1,0:T(8,128)(2,1)S(1)}, u32[]{:S(2)}, u32[]{:S(2)}) collective-permute-start(bf16[1,768,256]{2,1,0:T(8,128)(2,1)S(1)} %slice.128), channel_id=1, source_target_pairs={{0,16},{4,20},{8,24},{12,28},{16,0},{20,4},{24,8},{28,12},{1,17},{... | collective-permute-start | bytes 1179656 | tf_op jit(solution)/shard_map/ppermute | solution.py:17
  163.4 4.2 %collective-permute-done.23 = bf16[2,256,768]{2,1,0:T(8,128)(2,1)S(1)} collective-permute-done((bf16[2,256,768]{2,1,0:T(8,128)(2,1)S(1)}, bf16[2,256,768]{2,1,0:T(8,128)(2,1)S(1)}, u32[]{:S(2)}, u32[]{:S(2)}) %collective-permute-start.23) | collective-permute-done | bytes 786464 | tf_op jit(solution)/shard_map/ppermute | solution.py:17
  167.8 2.7 %collective-permute-start.25 = (bf16[1,256,768]{2,1,0:T(8,128)(2,1)S(1)}, bf16[1,256,768]{2,1,0:T(8,128)(2,1)S(1)}, u32[]{:S(2)}, u32[]{:S(2)}) collective-permute-start(bf16[1,256,768]{2,1,0:T(8,128)(2,1)S(1)} %slice.127), channel_id=1, source_target_pairs={{0,16},{4,20},{8,24},{12,28},{16,0},{20,4},{24,8},{28,12},{1,17},{... | collective-permute-start | bytes 1179656 | tf_op jit(solution)/shard_map/ppermute | solution.py:17
  170.5 21.7 %collective-permute-done.22 = bf16[2,256,768]{2,1,0:T(8,128)(2,1)S(1)} collective-permute-done((bf16[2,256,768]{2,1,0:T(8,128)(2,1)S(1)}, bf16[2,256,768]{2,1,0:T(8,128)(2,1)S(1)}, u32[]{:S(2)}, u32[]{:S(2)}) %collective-permute-start.22) | collective-permute-done | bytes 786464 | tf_op jit(solution)/shard_map/ppermute | solution.py:17
  193.7 1.0 fusion
  194.6 12.0 %collective-permute-done.25 = bf16[1,256,768]{2,1,0:T(8,128)(2,1)S(1)} collective-permute-done((bf16[1,256,768]{2,1,0:T(8,128)(2,1)S(1)}, bf16[1,256,768]{2,1,0:T(8,128)(2,1)S(1)}, u32[]{:S(2)}, u32[]{:S(2)}) %collective-permute-start.25) | collective-permute-done | bytes 393248 | tf_op jit(solution)/shard_map/ppermute | solution.py:17
  206.6 7.4 %collective-permute-done.24 = bf16[1,256,768]{2,1,0:T(8,128)(2,1)S(1)} collective-permute-done((bf16[1,256,768]{2,1,0:T(8,128)(2,1)S(1)}, bf16[1,256,768]{2,1,0:T(8,128)(2,1)S(1)}, u32[]{:S(2)}, u32[]{:S(2)}) %collective-permute-start.24) | collective-permute-done | bytes 393248 | tf_op jit(solution)/shard_map/ppermute | solution.py:17
  214.0 1.3 fusion.1
  (103 shorter events, 12.0 us)
Async XLA Ops:
  0.6 6.2 %collective-permute-start.3 = (bf16[192,2048]{1,0:T(8,128)(2,1)}, bf16[192,2048]{1,0:T(8,128)(2,1)S(1)}, u32[]{:S(2)}, u32[]{:S(2)}) collective-permute-start(bf16[192,2048]{1,0:T(8,128)(2,1)} %refs_0_.7), channel_id=1, source_target_pairs={{0,1},{1,0},{2,3},{3,2},{4,5},{5,4},{6,7},{7,6},{8,9},{9,8},{10,11... | collective-permute-start | bytes 2359304 | tf_op jit(solution)/shard_map/ppermute | solution.py:17
  1.2 20.9 %collective-permute-start.4 = (bf16[192,2048]{1,0:T(8,128)(2,1)}, bf16[192,2048]{1,0:T(8,128)(2,1)S(1)}, u32[]{:S(2)}, u32[]{:S(2)}) collective-permute-start(bf16[192,2048]{1,0:T(8,128)(2,1)} %refs_0_.7), channel_id=1, source_target_pairs={{0,2},{1,3},{2,0},{3,1},{4,6},{5,7},{6,4},{7,5},{8,10},{9,11},{10,... | collective-permute-start | bytes 2359304 | tf_op jit(solution)/shard_map/ppermute | solution.py:17
  5.3 1.5 copy-start.16
  5.3 1.5 collective-permute-start
  6.8 0.9 copy-start.3
  22.1 17.2 %copy-start.4 = (bf16[192,2048]{1,0:T(8,128)(2,1)}, bf16[192,2048]{1,0:T(8,128)(2,1)S(1)}, u32[]{:S(2)}) copy-start(bf16[192,2048]{1,0:T(8,128)(2,1)S(1)} %collective-permute-done.4.refs_2_) | copy-start | bytes 2359300
  22.1 27.5 %collective-permute-start.5 = (bf16[192,2048]{1,0:T(8,128)(2,1)S(1)}, bf16[192,2048]{1,0:T(8,128)(2,1)S(1)}, u32[]{:S(2)}, u32[]{:S(2)}) collective-permute-start(bf16[192,2048]{1,0:T(8,128)(2,1)S(1)} %collective-permute-done.4.refs_2_), channel_id=1, source_target_pairs={{0,1},{1,0},{2,3},{3,2},{4,5},{5,4},{6,7},{7,6},{8,9},{9,8},{10,11... | collective-permute-start | bytes 2359304 | tf_op jit(solution)/shard_map/ppermute | solution.py:17
  24.7 5.2 %collective-permute-start.1 = (bf16[192,1024]{1,0:T(8,128)(2,1)}, bf16[192,1024]{1,0:T(8,128)(2,1)S(1)}, u32[]{:S(2)}, u32[]{:S(2)}) collective-permute-start(bf16[192,1024]{1,0:T(8,128)(2,1)} %shard_map.119.refs_2_.refs_0_), channel_id=1, source_target_pairs={{0,1},{1,0},{2,3},{3,2},{4,5},{5,4},{6,7},{7,6},{8,9},{9,8},{10,11... | collective-permute-start | bytes 1179656 | tf_op jit(solution)/shard_map/ppermute | solution.py:17
  27.8 3.8 %collective-permute-start.2 = (bf16[192,1024]{1,0:T(8,128)(2,1)}, bf16[192,1024]{1,0:T(8,128)(2,1)S(1)}, u32[]{:S(2)}, u32[]{:S(2)}) collective-permute-start(bf16[192,1024]{1,0:T(8,128)(2,1)} %shard_map.120.refs_3_.refs_0_), channel_id=1, source_target_pairs={{0,1},{1,0},{2,3},{3,2},{4,5},{5,4},{6,7},{7,6},{8,9},{9,8},{10,11... | collective-permute-start | bytes 1179656 | tf_op jit(solution)/shard_map/ppermute | solution.py:17
  27.8 12.2 %collective-permute-start.8 = (bf16[192,1024]{1,0:T(8,128)(2,1)}, bf16[192,1024]{1,0:T(8,128)(2,1)S(1)}, u32[]{:S(2)}, u32[]{:S(2)}) collective-permute-start(bf16[192,1024]{1,0:T(8,128)(2,1)} %shard_map.119.refs_2_.refs_0_), channel_id=1, source_target_pairs={{0,2},{1,3},{2,0},{3,1},{4,6},{5,7},{6,4},{7,5},{8,10},{9,11},{10,... | collective-permute-start | bytes 1179656 | tf_op jit(solution)/shard_map/ppermute | solution.py:17
  29.6 29.3 %collective-permute-start.9 = (bf16[192,1024]{1,0:T(8,128)(2,1)}, bf16[192,1024]{1,0:T(8,128)(2,1)S(1)}, u32[]{:S(2)}, u32[]{:S(2)}) collective-permute-start(bf16[192,1024]{1,0:T(8,128)(2,1)} %shard_map.120.refs_3_.refs_0_), channel_id=1, source_target_pairs={{0,2},{1,3},{2,0},{3,1},{4,6},{5,7},{6,4},{7,5},{8,10},{9,11},{10,... | collective-permute-start | bytes 1179656 | tf_op jit(solution)/shard_map/ppermute | solution.py:17
  29.9 1.8 copy-start.14
  29.9 19.6 %collective-permute-start.6 = (bf16[192,4]{1,0:T(8,128)(2,1)}, bf16[192,4]{1,0:T(8,128)(2,1)S(1)}, u32[]{:S(2)}, u32[]{:S(2)}) collective-permute-start(bf16[192,4]{1,0:T(8,128)(2,1)} %copy-done.16), channel_id=1, source_target_pairs={{0,2},{1,3},{2,0},{3,1},{4,6},{5,7},{6,4},{7,5},{8,10},{9,11},{10,... | collective-permute-start | bytes 4616 | tf_op jit(solution)/shard_map/ppermute | solution.py:17
  31.6 18.0 %collective-permute-start.7 = (bf16[192,4]{1,0:T(8,128)(2,1)}, bf16[192,4]{1,0:T(8,128)(2,1)S(1)}, u32[]{:S(2)}, u32[]{:S(2)}) collective-permute-start(bf16[192,4]{1,0:T(8,128)(2,1)} %copy-done.16), channel_id=1, source_target_pairs={{0,3},{1,2},{2,1},{3,0},{4,7},{5,6},{6,5},{7,4},{8,11},{9,10},{10,... | collective-permute-start | bytes 4616 | tf_op jit(solution)/shard_map/ppermute | solution.py:17
  40.0 19.2 %copy-start.13 = (bf16[192,1024]{1,0:T(8,128)(2,1)}, bf16[192,1024]{1,0:T(8,128)(2,1)S(1)}, u32[]{:S(2)}) copy-start(bf16[192,1024]{1,0:T(8,128)(2,1)S(1)} %collective-permute-done.8.refs_2_) | copy-start | bytes 1179652
  40.0 19.2 %collective-permute-start.10 = (bf16[192,1024]{1,0:T(8,128)(2,1)S(1)}, bf16[192,1024]{1,0:T(8,128)(2,1)S(1)}, u32[]{:S(2)}, u32[]{:S(2)}) collective-permute-start(bf16[192,1024]{1,0:T(8,128)(2,1)S(1)} %collective-permute-done.8.refs_2_), channel_id=1, source_target_pairs={{0,1},{1,0},{2,3},{3,2},{4,5},{5,4},{6,7},{7,6},{8,9},{9,8},{10,11... | collective-permute-start | bytes 1179656 | tf_op jit(solution)/shard_map/ppermute | solution.py:17
  50.3 0.9 copy-start.5
  58.9 8.7 %copy-start.10 = (bf16[192,1024]{1,0:T(8,128)(2,1)}, bf16[192,1024]{1,0:T(8,128)(2,1)S(1)}, u32[]{:S(2)}) copy-start(bf16[192,1024]{1,0:T(8,128)(2,1)S(1)} %collective-permute-done.9.refs_3_.refs_2_) | copy-start | bytes 1179652
  58.9 8.6 %collective-permute-start.11 = (bf16[192,1024]{1,0:T(8,128)(2,1)S(1)}, bf16[192,1024]{1,0:T(8,128)(2,1)S(1)}, u32[]{:S(2)}, u32[]{:S(2)}) collective-permute-start(bf16[192,1024]{1,0:T(8,128)(2,1)S(1)} %collective-permute-done.9.refs_3_.refs_2_), channel_id=1, source_target_pairs={{0,1},{1,0},{2,3},{3,2},{4,5},{5,4},{6,7},{7,6},{8,9},{9,8},{10,11... | collective-permute-start | bytes 1179656 | tf_op jit(solution)/shard_map/ppermute | solution.py:17
  59.3 0.8 copy-start.15
  65.8 61.3 %collective-permute-start.16 = (bf16[4,768,256]{2,1,0:T(8,128)(2,1)}, bf16[4,768,256]{2,1,0:T(8,128)(2,1)}, u32[]{:S(2)}, u32[]{:S(2)}) collective-permute-start(bf16[4,768,256]{2,1,0:T(8,128)(2,1)} %shard_map.124), channel_id=1, source_target_pairs={{0,4},{4,0},{8,12},{12,8},{16,20},{20,16},{24,28},{28,24},{1,5},{5... | collective-permute-start | bytes 4718600 | tf_op jit(solution)/shard_map/ppermute | solution.py:17
  86.6 6.4 %copy-start.8 = (bf16[384,768]{1,0:T(8,128)(2,1)S(1)}, bf16[384,768]{1,0:T(8,128)(2,1)}, u32[]{:S(2)}) copy-start(bf16[384,768]{1,0:T(8,128)(2,1)} %get-tuple-element.58.refs_5_) | copy-start | bytes 1769476
  93.0 5.5 %copy-start.7 = (bf16[384,768]{1,0:T(8,128)(2,1)S(1)}, bf16[384,768]{1,0:T(8,128)(2,1)}, u32[]{:S(2)}) copy-start(bf16[384,768]{1,0:T(8,128)(2,1)} %get-tuple-element.60.refs_4_) | copy-start | bytes 1769476
  93.0 5.5 %copy-start.23 = (bf16[1,2048,768]{2,1,0:T(8,128)(2,1)S(1)}, bf16[1,2048,768]{2,1,0:T(8,128)(2,1)}, u32[]{:S(2)}) copy-start(bf16[1,2048,768]{2,1,0:T(8,128)(2,1)} %param.13) | copy-start | bytes 9437188
  97.5 4.2 %copy-start.12 = (bf16[384,2048]{1,0:T(8,128)(2,1)}, bf16[384,2048]{1,0:T(8,128)(2,1)S(1)}, u32[]{:S(2)}) copy-start(bf16[384,2048]{1,0:T(8,128)(2,1)S(1)} %add_convert_fusion) | copy-start | bytes 4718596
  98.5 3.1 %copy-start.17 = (bf16[384,1]{1,0:T(8,128)(2,1)S(1)}, bf16[384,1]{1,0:T(8,128)(2,1)}, u32[]{:S(2)}) copy-start(bf16[384,1]{1,0:T(8,128)(2,1)} %get-tuple-element.65) | copy-start | bytes 2308
  98.5 5.4 %copy-start.18 = (bf16[384,1]{1,0:T(8,128)(2,1)S(1)}, bf16[384,1]{1,0:T(8,128)(2,1)}, u32[]{:S(2)}) copy-start(bf16[384,1]{1,0:T(8,128)(2,1)} %get-tuple-element.67) | copy-start | bytes 2308
  98.5 26.4 %collective-permute-start.13 = (bf16[192,2048]{1,0:T(8,128)(2,1)}, bf16[192,2048]{1,0:T(8,128)(2,1)}, u32[]{:S(2)}, u32[]{:S(2)}) collective-permute-start(bf16[192,2048]{1,0:T(8,128)(2,1)} %slice.89), channel_id=1, source_target_pairs={{0,1},{1,0},{2,3},{3,2},{4,5},{5,4},{6,7},{7,6},{8,9},{9,8},{10,11... | collective-permute-start | bytes 2359304 | tf_op jit(solution)/shard_map/ppermute | solution.py:17
  101.7 54.2 %collective-permute-start.20 = (bf16[4,256,768]{2,1,0:T(8,128)(2,1)}, bf16[4,256,768]{2,1,0:T(8,128)(2,1)}, u32[]{:S(2)}, u32[]{:S(2)}) collective-permute-start(bf16[4,256,768]{2,1,0:T(8,128)(2,1)} %shard_map.127), channel_id=1, source_target_pairs={{0,4},{4,0},{8,12},{12,8},{16,20},{20,16},{24,28},{28,24},{1,5},{5... | collective-permute-start | bytes 4718600 | tf_op jit(solution)/shard_map/ppermute | solution.py:17
  102.1 37.6 %collective-permute-start.15 = (bf16[4,256,768]{2,1,0:T(8,128)(2,1)}, bf16[4,256,768]{2,1,0:T(8,128)(2,1)}, u32[]{:S(2)}, u32[]{:S(2)}) collective-permute-start(bf16[4,256,768]{2,1,0:T(8,128)(2,1)} %shard_map.126), channel_id=1, source_target_pairs={{0,8},{4,12},{8,0},{12,4},{16,24},{20,28},{24,16},{28,20},{1,9},{5... | collective-permute-start | bytes 4718600 | tf_op jit(solution)/shard_map/ppermute | solution.py:17
  103.9 43.1 %collective-permute-start.18 = (bf16[192,1]{1,0:T(8,128)(2,1)S(1)}, bf16[192,1]{1,0:T(8,128)(2,1)S(1)}, u32[]{:S(2)}, u32[]{:S(2)}) collective-permute-start(bf16[192,1]{1,0:T(8,128)(2,1)S(1)} %get-tuple-element.77), channel_id=1, source_target_pairs={{0,2},{1,3},{2,0},{3,1},{4,6},{5,7},{6,4},{7,5},{8,10},{9,11},{10,... | collective-permute-start | bytes 1160 | tf_op jit(solution)/shard_map/ppermute | solution.py:17
  118.1 9.1 %copy-start = (f32[4,768,256]{2,1,0:T(8,128)S(1)}, f32[4,768,256]{2,1,0:T(8,128)}, u32[]{:S(2)}) copy-start(f32[4,768,256]{2,1,0:T(8,128)} %shard_map.128) | copy-start | bytes 9437188
  126.6 3.0 %copy-start.6 = (bf16[384,768]{1,0:T(8,128)(2,1)S(1)}, bf16[384,768]{1,0:T(8,128)(2,1)}, u32[]{:S(2)}) copy-start(bf16[384,768]{1,0:T(8,128)(2,1)} %get-tuple-element.57.refs_4_) | copy-start | bytes 1769476
  126.6 3.0 %copy-start.24 = (bf16[1,2048,768]{2,1,0:T(8,128)(2,1)S(1)}, bf16[1,2048,768]{2,1,0:T(8,128)(2,1)}, u32[]{:S(2)}) copy-start(bf16[1,2048,768]{2,1,0:T(8,128)(2,1)} %param.12) | copy-start | bytes 9437188
  126.6 3.5 %copy-start.25 = (f32[384,2048]{1,0:T(8,128)S(1)}, f32[384,2048]{1,0:T(8,128)}, u32[]{:S(2)}) copy-start(f32[384,2048]{1,0:T(8,128)} %fusion.9) | copy-start | bytes 9437188
  126.6 22.9 %collective-permute-start.14 = (bf16[192,2048]{1,0:T(8,128)(2,1)S(1)}, bf16[192,2048]{1,0:T(8,128)(2,1)S(1)}, u32[]{:S(2)}, u32[]{:S(2)}) collective-permute-start(bf16[192,2048]{1,0:T(8,128)(2,1)S(1)} %add_convert_fusion.3), channel_id=1, source_target_pairs={{0,2},{1,3},{2,0},{3,1},{4,6},{5,7},{6,4},{7,5},{8,10},{9,11},{10,... | collective-permute-start | bytes 2359304 | tf_op jit(solution)/shard_map/ppermute | solution.py:17
  129.3 10.3 %copy-start.2 = (f32[4,256,768]{2,1,0:T(8,128)S(1)}, f32[4,256,768]{2,1,0:T(8,128)}, u32[]{:S(2)}) copy-start(f32[4,256,768]{2,1,0:T(8,128)} %shard_map.129) | copy-start | bytes 9437188
  129.3 26.4 %collective-permute-start.21 = (bf16[2,768,256]{2,1,0:T(8,128)(2,1)S(1)}, bf16[2,768,256]{2,1,0:T(8,128)(2,1)S(1)}, u32[]{:S(2)}, u32[]{:S(2)}) collective-permute-start(bf16[2,768,256]{2,1,0:T(8,128)(2,1)S(1)} %slice.125), channel_id=1, source_target_pairs={{0,8},{4,12},{8,0},{12,4},{16,24},{20,28},{24,16},{28,20},{1,9},{5... | collective-permute-start | bytes 2359304 | tf_op jit(solution)/shard_map/ppermute | solution.py:17
  139.7 5.8 %collective-permute-start.19 = (bf16[192,1]{1,0:T(8,128)(2,1)S(1)}, bf16[192,1]{1,0:T(8,128)(2,1)S(1)}, u32[]{:S(2)}, u32[]{:S(2)}) collective-permute-start(bf16[192,1]{1,0:T(8,128)(2,1)S(1)} %get-tuple-element.78), channel_id=1, source_target_pairs={{0,3},{1,2},{2,1},{3,0},{4,7},{5,6},{6,5},{7,4},{8,11},{9,10},{10,... | collective-permute-start | bytes 1160 | tf_op jit(solution)/shard_map/ppermute | solution.py:17
  141.4 14.6 %copy-start.1 = (f32[4,256,768]{2,1,0:T(8,128)S(1)}, f32[4,256,768]{2,1,0:T(8,128)}, u32[]{:S(2)}) copy-start(f32[4,256,768]{2,1,0:T(8,128)} %shard_map.130) | copy-start | bytes 9437188
  145.5 2.3 %collective-permute-start.17 = (bf16[192,1]{1,0:T(8,128)(2,1)S(1)}, bf16[192,1]{1,0:T(8,128)(2,1)S(1)}, u32[]{:S(2)}, u32[]{:S(2)}) collective-permute-start(bf16[192,1]{1,0:T(8,128)(2,1)S(1)} %slice.73), channel_id=1, source_target_pairs={{0,1},{1,0},{2,3},{3,2},{4,5},{5,4},{6,7},{7,6},{8,9},{9,8},{10,11... | collective-permute-start | bytes 1160 | tf_op jit(solution)/shard_map/ppermute | solution.py:17
  147.0 12.6 %collective-permute-start.12 = (bf16[192,2048]{1,0:T(8,128)(2,1)S(1)}, bf16[192,2048]{1,0:T(8,128)(2,1)S(1)}, u32[]{:S(2)}, u32[]{:S(2)}) collective-permute-start(bf16[192,2048]{1,0:T(8,128)(2,1)S(1)} %slice.87), channel_id=1, source_target_pairs={{0,1},{1,0},{2,3},{3,2},{4,5},{5,4},{6,7},{7,6},{8,9},{9,8},{10,11... | collective-permute-start | bytes 2359304 | tf_op jit(solution)/shard_map/ppermute | solution.py:17
  147.8 19.8 %collective-permute-start.23 = (bf16[2,256,768]{2,1,0:T(8,128)(2,1)S(1)}, bf16[2,256,768]{2,1,0:T(8,128)(2,1)S(1)}, u32[]{:S(2)}, u32[]{:S(2)}) collective-permute-start(bf16[2,256,768]{2,1,0:T(8,128)(2,1)S(1)} %slice.124), channel_id=1, source_target_pairs={{0,4},{4,0},{8,12},{12,8},{16,20},{20,16},{24,28},{28,24},{1,5},{5... | collective-permute-start | bytes 2359304 | tf_op jit(solution)/shard_map/ppermute | solution.py:17
  157.8 34.4 %collective-permute-start.22 = (bf16[2,256,768]{2,1,0:T(8,128)(2,1)S(1)}, bf16[2,256,768]{2,1,0:T(8,128)(2,1)S(1)}, u32[]{:S(2)}, u32[]{:S(2)}) collective-permute-start(bf16[2,256,768]{2,1,0:T(8,128)(2,1)S(1)} %slice.123), channel_id=1, source_target_pairs={{0,8},{4,12},{8,0},{12,4},{16,24},{20,28},{24,16},{28,20},{1,9},{5... | collective-permute-start | bytes 2359304 | tf_op jit(solution)/shard_map/ppermute | solution.py:17
  160.9 32.8 %collective-permute-start.26 = (bf16[1,768,256]{2,1,0:T(8,128)(2,1)S(1)}, bf16[1,768,256]{2,1,0:T(8,128)(2,1)S(1)}, u32[]{:S(2)}, u32[]{:S(2)}) collective-permute-start(bf16[1,768,256]{2,1,0:T(8,128)(2,1)S(1)} %slice.128), channel_id=1, source_target_pairs={{0,16},{4,20},{8,24},{12,28},{16,0},{20,4},{24,8},{28,12},{1,17},{... | collective-permute-start | bytes 1179656 | tf_op jit(solution)/shard_map/ppermute | solution.py:17
  167.8 25.3 %copy-start.22 = (s32[192,2]{0,1:T(2,128)S(1)}, s32[192,2]{0,1:T(2,128)}, u32[]{:S(2)}) copy-start(s32[192,2]{0,1:T(2,128)} %param.10) | copy-start | bytes 4612
  167.8 38.7 %collective-permute-start.25 = (bf16[1,256,768]{2,1,0:T(8,128)(2,1)S(1)}, bf16[1,256,768]{2,1,0:T(8,128)(2,1)S(1)}, u32[]{:S(2)}, u32[]{:S(2)}) collective-permute-start(bf16[1,256,768]{2,1,0:T(8,128)(2,1)S(1)} %slice.127), channel_id=1, source_target_pairs={{0,16},{4,20},{8,24},{12,28},{16,0},{20,4},{24,8},{28,12},{1,17},{... | collective-permute-start | bytes 1179656 | tf_op jit(solution)/shard_map/ppermute | solution.py:17
  192.4 21.6 %collective-permute-start.24 = (bf16[1,256,768]{2,1,0:T(8,128)(2,1)S(1)}, bf16[1,256,768]{2,1,0:T(8,128)(2,1)S(1)}, u32[]{:S(2)}, u32[]{:S(2)}) collective-permute-start(bf16[1,256,768]{2,1,0:T(8,128)(2,1)S(1)} %slice.126), channel_id=1, source_target_pairs={{0,16},{4,20},{8,24},{12,28},{16,0},{20,4},{24,8},{28,12},{1,17},{... | collective-permute-start | bytes 1179656 | tf_op jit(solution)/shard_map/ppermute | solution.py:17
  (5 other events, 3.4 us)

commit v2 on v1

v2 whole, which is shorter than its diff:
```python
import jax
import jax.numpy as jnp
from jax import lax
from jax.experimental import pallas as pl
from jax.experimental.pallas import tpu as pltpu
from jax.sharding import PartitionSpec as P


F32 = jnp.float32
BF16 = jnp.bfloat16
ROWS = (((0,), (0,)), ((), ()))
COLS = (((1,), (1,)), ((), ()))


def swap(value, axis, mask):
    count = lax.axis_size(axis)
    return lax.ppermute(value, axis, [(i, i ^ mask) for i in range(count)])


def after(value, *earlier):
    return lax.optimization_barrier((value,) + earlier)[0]


def lane_block(size, most=256):
    return most if size % most == 0 else size


def pick_columns(scalars, masks, value, width):
    rows, count = value.shape[0], len(masks)

    def kernel(scalar_ref, in_ref, out_ref):
        for k, mask in enumerate(masks):
            start = pl.multiple_of((scalar_ref[1] ^ mask) * width, width)
            out_ref[:, k * width : (k + 1) * width] = in_ref[:, pl.ds(start, width)]

    return pl.pallas_call(
        kernel,
        grid_spec=pltpu.PrefetchScalarGridSpec(
            num_scalar_prefetch=1,
            grid=(1,),
            in_specs=[pl.BlockSpec(value.shape, lambda k, t: (0, 0))],
            out_specs=pl.BlockSpec((rows, count * width), lambda k, t: (0, 0)),
        ),
        out_shape=jax.ShapeDtypeStruct((rows, count * width), value.dtype),
    )(scalars, value)


def prob_of(coef_refs, expert):
    parts = []
    for ref in coef_refs:
        lanes = lax.broadcasted_iota(jnp.int32, ref.shape, 1)
        parts.append(jnp.where(lanes == expert, ref[...].astype(F32), 0.0))
    return jnp.sum(jnp.concatenate(parts, axis=0), axis=1, keepdims=True)


def activations(expert, coefs, tokens, gate_w, up_w):
    rows, width = tokens[0].shape
    hidden = gate_w.shape[1]
    total = rows * len(tokens)
    block = lane_block(hidden)
    count = len(tokens)

    def kernel(expert_ref, *refs):
        coef_refs, token_refs = refs[:count], refs[count : 2 * count]
        gate_ref, up_ref, gate_out, up_out, weighted_out, rows_ref = refs[2 * count :]

        @pl.when(pl.program_id(0) == 0)
        def _():
            for j, ref in enumerate(token_refs):
                rows_ref[j * rows : (j + 1) * rows, :] = ref[...]

        x = rows_ref[...]
        gate = jnp.dot(x, gate_ref[...], preferred_element_type=F32)
        up = jnp.dot(x, up_ref[...], preferred_element_type=F32)
        gate_out[...] = gate
        up_out[...] = up
        activation = gate * jax.nn.sigmoid(gate) * up
        weighted_out[...] = (prob_of(coef_refs, expert_ref[0]) * activation).astype(BF16)

    whole = [pl.BlockSpec(c.shape, lambda k, e: (0, 0)) for c in coefs]
    whole += [pl.BlockSpec(t.shape, lambda k, e: (0, 0)) for t in tokens]
    column = pl.BlockSpec((width, block), lambda k, e: (0, k))
    out = pl.BlockSpec((total, block), lambda k, e: (0, k))
    return pl.pallas_call(
        kernel,
        grid_spec=pltpu.PrefetchScalarGridSpec(
            num_scalar_prefetch=1,
            grid=(hidden // block,),
            in_specs=whole + [column, column],
            out_specs=[out, out, out],
            scratch_shapes=[pltpu.VMEM((total, width), BF16)],
        ),
        out_shape=[
            jax.ShapeDtypeStruct((total, hidden), F32),
            jax.ShapeDtypeStruct((total, hidden), F32),
            jax.ShapeDtypeStruct((total, hidden), BF16),
        ],
        cost_estimate=pl.CostEstimate(
            flops=4 * total * width * hidden, bytes_accessed=4 * width * hidden, transcendentals=0
        ),
    )(expert, *coefs, *tokens, gate_w, up_w)


def hidden_grads(scalars, coefs, parts, masks, down_w, gate_act, up_act, own_width):
    rows = parts[0][0].shape[0]
    hidden, width = down_w.shape
    total = rows * len(parts)
    block = lane_block(hidden)
    count = len(parts)
    flat = [part for pair in parts for part in pair]
    groups = len(gate_act)
    per_row = len(parts[0])

    def kernel(scalar_ref, *refs):
        coef_refs, part_refs = refs[:count], refs[count : count + len(flat)]
        rest = refs[count + len(flat) :]
        down_ref, gate_refs, up_refs = rest[0], rest[1 : 1 + groups], rest[1 + groups : 1 + 2 * groups]
        gate_out, up_out, prob_out, rows_ref, sum_ref = rest[1 + 2 * groups :]
        step = pl.program_id(0)

        @pl.when(step == 0)
        def _():
            for i, ref in enumerate(part_refs):
                j, h = divmod(i, per_row)
                blocks = ref.shape[1] // own_width
                for b in range(blocks):
                    owner = scalar_ref[1] ^ masks[h * blocks + b]
                    start = pl.multiple_of(owner * own_width, own_width)
                    rows_ref[j * rows : (j + 1) * rows, pl.ds(start, own_width)] = ref[
                        :, b * own_width : (b + 1) * own_width
                    ]
            sum_ref[...] = jnp.zeros_like(sum_ref)

        back = lax.dot_general(rows_ref[...], down_ref[...], COLS, preferred_element_type=F32)
        gate = jnp.concatenate([r[...] for r in gate_refs], axis=0)
        up = jnp.concatenate([r[...] for r in up_refs], axis=0)
        s = jax.nn.sigmoid(gate)
        silu = gate * s
        sum_ref[...] += jnp.sum(silu * up * back, axis=1, keepdims=True)
        act_grad = prob_of(coef_refs, scalar_ref[0]) * back
        gate_out[...] = (act_grad * up * s * (1.0 + gate * (1.0 - s))).astype(BF16)
        up_out[...] = (act_grad * silu).astype(BF16)

        @pl.when(step == pl.num_programs(0) - 1)
        def _():
            prob_out[...] = sum_ref[...].astype(BF16)

    whole = [pl.BlockSpec(c.shape, lambda k, e: (0, 0)) for c in coefs]
    whole += [pl.BlockSpec(t.shape, lambda k, e: (0, 0)) for t in flat]
    column = pl.BlockSpec((total, block), lambda k, e: (0, k))
    some = [pl.BlockSpec((a.shape[0], block), lambda k, e: (0, k)) for a in gate_act + up_act]
    return pl.pallas_call(
        kernel,
        grid_spec=pltpu.PrefetchScalarGridSpec(
            num_scalar_prefetch=1,
            grid=(hidden // block,),
            in_specs=whole + [pl.BlockSpec((block, width), lambda k, e: (k, 0))] + some,
            out_specs=[column, column, pl.BlockSpec((total, 1), lambda k, e: (0, 0))],
            scratch_shapes=[pltpu.VMEM((total, width), BF16), pltpu.VMEM((total, 1), F32)],
        ),
        out_shape=[
            jax.ShapeDtypeStruct((total, hidden), BF16),
            jax.ShapeDtypeStruct((total, hidden), BF16),
            jax.ShapeDtypeStruct((total, 1), BF16),
        ],
        cost_estimate=pl.CostEstimate(
            flops=2 * total * width * hidden, bytes_accessed=2 * width * hidden, transcendentals=0
        ),
    )(scalars, *coefs, *flat, down_w, *gate_act, *up_act)


def weight_blocks(scalars, masks, rows, grads, own_width, flip, dtype):
    pieces, count = len(masks), len(masks[0])
    hidden = grads[0].shape[1]
    width = hidden // pieces
    piece = (width, own_width) if flip else (own_width, width)
    same = all(m == masks[0] for m in masks)

    def kernel(scalar_ref, *refs):
        row_refs, grad_refs = refs[: len(rows)], refs[len(rows) : len(rows) + len(grads)]
        out_refs = refs[len(rows) + len(grads) :]
        grad = jnp.concatenate([g[...] for g in grad_refs], axis=0)

        def block(k, mask, grad):
            start = k * own_width if flip else (scalar_ref[1] ^ mask) * own_width
            lanes = pl.ds(pl.multiple_of(start, own_width), own_width)
            x = jnp.concatenate([r[:, lanes] for r in row_refs], axis=0)
            pair = (grad, x) if flip else (x, grad)
            return lax.dot_general(*pair, ROWS, preferred_element_type=F32).astype(dtype)

        for k in range(count):
            if same:
                acc = block(k, masks[0][k], grad)
            for i, ref in enumerate(out_refs):
                units = slice(i * width, (i + 1) * width)
                if not same:
                    ref[k] = block(k, masks[i][k], grad[:, units])
                else:
                    ref[k] = acc if pieces == 1 else acc[:, units]

    vmem = pl.BlockSpec(memory_space=pltpu.VMEM)
    return pl.pallas_call(
        kernel,
        in_specs=[pl.BlockSpec(memory_space=pltpu.SMEM)] + [vmem] * (len(rows) + len(grads)),
        out_specs=[vmem] * pieces,
        out_shape=[jax.ShapeDtypeStruct((count,) + piece, dtype)] * pieces,
        cost_estimate=pl.CostEstimate(
            flops=2 * count * own_width * hidden * rows[0].shape[0] * len(rows),
            bytes_accessed=2 * count * own_width * rows[0].shape[0] * len(rows),
            transcendentals=0,
        ),
    )(scalars, *rows, *grads)


def masks_of(bits):
    masks = [0]
    for bit in reversed(bits):
        masks = [bit | m for m in masks] + masks
    return masks


def step(tokens, upstream, route_ids, route_probs, gate_proj, up_proj, down_proj):
    ep_count = lax.axis_size("ep")
    rep_count = lax.axis_size("rep")
    ep_index = lax.axis_index("ep")
    rep_index = lax.axis_index("rep")
    tok_rows, model_width = tokens.shape
    own_width = model_width // rep_count
    gate_w, up_w, down_w = gate_proj[0], up_proj[0], down_proj[0]
    bits = [1 << i for i in range(rep_count.bit_length() - 1)]
    turned = [bits[1], bits[0]] + bits[2:]
    near_masks, turned_masks = masks_of(bits[1:]), masks_of(turned[1:])
    far_masks, turned_far_masks = [bits[0] | m for m in near_masks], [turned[0] | m for m in turned_masks]
    chip_masks = list(range(0, ep_count, 2))

    scalars = jnp.stack([ep_index, rep_index]).astype(jnp.int32)

    def across(value):
        blocks = {}
        for mask in chip_masks[1:]:
            blocks[mask] = swap(value, "ep", mask)
        blocks[0], blocks[1] = value, swap(value, "ep", 1)
        return blocks

    def forward(blocks, *earlier):
        for mask in chip_masks[1:]:
            blocks[mask] = after(blocks[mask], *earlier)
            blocks[mask | 1] = swap(blocks[mask], "ep", 1)

    token_rows = across(tokens)
    lanes = jnp.arange(ep_count, dtype=jnp.int32)
    coef = jnp.sum(
        jnp.where(route_ids[:, :, None] == lanes[None, None, :], route_probs[:, :, None].astype(F32), 0.0),
        axis=1,
    ).astype(BF16)
    coefs = {j: swap(coef, "ep", j) if j else coef for j in range(ep_count)}
    up_far = across(pick_columns(scalars, far_masks, upstream, own_width))
    up_near = across(pick_columns(scalars, near_masks, upstream, own_width))
    acts = {}

    def act(mask, *earlier):
        pair = (mask, mask | 1)
        rows = [token_rows[j] for j in pair]
        rows[0] = after(rows[0], *earlier)
        acts[mask] = activations(scalars, [coefs[j] for j in pair], rows, gate_w, up_w)

    act(0)
    forward(token_rows, acts[0][0])
    for mask in chip_masks[1:]:
        act(mask, acts[0][0])
    forward(up_far, acts[chip_masks[-1]][0])
    up_far_list = [up_far[j] for j in range(ep_count)]
    token_list = [token_rows[j] for j in range(ep_count)]
    weighted = [acts[mask][2] for mask in chip_masks]

    def outer(masks, rows, grad, flip, dtype, *earlier):
        grad = [after(grad[0], *earlier)] + grad[1:] if earlier else grad
        return weight_blocks(scalars, masks, rows, grad, own_width, flip, dtype)

    state = {}

    def send_first(name, values, *orders):
        for i, (value, order) in enumerate(zip(values, orders)):
            state[name, i] = [swap(value, "rep", order[0]), None, order, 0]

    down_send = outer([far_masks], up_far_list, weighted, True, BF16)
    send_first("down", down_send, bits)
    forward(up_near, up_far[1])
    up_near_list = [up_near[j] for j in range(ep_count)]
    gate_acts = [acts[mask][0] for mask in chip_masks]
    gate_acts[0] = after(gate_acts[0], down_send[0])
    gate_grad, up_grad, prob_grad = hidden_grads(
        scalars,
        [coefs[j] for j in range(ep_count)],
        list(zip(up_far_list, up_near_list)),
        far_masks + near_masks,
        down_w,
        gate_acts,
        [acts[mask][1] for mask in chip_masks],
        own_width,
    )
    gate_grads, up_grads = [gate_grad], [up_grad]
    up_send = outer([turned_far_masks, far_masks], token_list, up_grads, False, BF16)
    send_first("up", up_send, turned, bits)
    gate_send = outer([far_masks] * 2, token_list, gate_grads, False, BF16, up_send[0])
    send_first("gate", gate_send, bits, bits)
    down_keep = outer([near_masks], up_near_list, weighted, True, F32, gate_send[0])

    done = [down_keep[0]]

    def advance(name, piece):
        got, keep, order, at = state[name, piece]
        got = after(got, done[0])
        if at + 1 == len(order):
            state[name, piece] = (keep + got.astype(F32)) * (1.0 / rep_count)
            return
        middle = keep.shape[0] // 2
        send = (keep[:middle] + got[:middle].astype(F32)).astype(BF16)
        rest = keep[middle:] + got[middle:].astype(F32)
        done[0] = send
        got = swap(send, "rep", order[at + 1])
        state[name, piece] = [got, rest, order, at + 1]

    def set_keep(name, values):
        for i, value in enumerate(values):
            state[name, i][1] = value
        done[0] = values[-1]

    set_keep("down", down_keep)
    advance("down", 0)
    set_keep("up", outer([turned_masks, near_masks], token_list, up_grads, False, F32, done[0]))
    advance("up", 0)
    set_keep("gate", outer([near_masks] * 2, token_list, gate_grads, False, F32, done[0]))
    advance("gate", 0)

    both = lax.dot_general(after(gate_grad, done[0]), gate_w, COLS, preferred_element_type=F32)
    both = both + lax.dot_general(after(up_grad, done[0]), up_w, COLS, preferred_element_type=F32)
    both = both.astype(BF16).reshape(ep_count, tok_rows, model_width)
    done[0] = both
    back = {mask: swap(both[mask | 1], "ep", 1) for mask in chip_masks}
    prob_blocks = after(prob_grad, done[0]).reshape(ep_count, tok_rows, 1)
    probs_back = [swap(prob_blocks[j], "ep", j) for j in range(1, ep_count)]
    advance("down", 0)
    sums = {}
    for mask in reversed(chip_masks):
        sums[mask] = both[mask].astype(F32) + after(back[mask], done[0]).astype(F32)
    far_sums = [swap(sums[mask].astype(BF16), "ep", mask) for mask in chip_masks[1:]]

    advance("gate", 1)
    advance("gate", 0)
    advance("gate", 1)
    advance("up", 1)
    token_sum = sums[0]
    for value in far_sums:
        token_sum = token_sum + after(value, done[0]).astype(F32)
    grad_tokens = token_sum.astype(BF16)
    grad_probs = 0.0
    for j, block in enumerate([prob_blocks[0]] + [after(p, done[0]) for p in probs_back]):
        grad_probs = grad_probs + jnp.where(route_ids == ep_index ^ j, block.astype(F32), 0.0)
    advance("up", 0)
    advance("up", 1)
    for _ in bits[2:]:
        for name, piece in (("down", 0), ("gate", 0), ("gate", 1), ("up", 0), ("up", 1)):
            advance(name, piece)

    def whole(name):
        return jnp.concatenate([value for key, value in state.items() if key[0] == name], axis=2)

    return (grad_tokens, grad_probs.astype(BF16), whole("gate"), whole("up"), whole("down"))


def solution(mesh):
    return jax.shard_map(
        step,
        mesh=mesh,
        in_specs=(
            P(("rep", "ep"), None),
            P(("rep", "ep"), None),
            P(("rep", "ep"), None),
            P(("rep", "ep"), None),
            P("ep", None, None),
            P("ep", None, None),
            P("ep", None, None),
        ),
        out_specs=(
            P(("rep", "ep"), None),
            P(("rep", "ep"), None),
            P("ep", "rep", None),
            P("ep", "rep", None),
            P("ep", None, "rep"),
        ),
        check_vma=False,
    )
```

time: 216 us -> 218 us (level)
  waiting for transfers between devices: 81.3 us -> 93.8 us
  Pallas kernels: 72.5 us -> 60.3 us
  starting transfers between devices: 24.9 us -> 31.9 us
  matrix products: 14.1 us -> 7.62 us
    ppermute x27 -> x33, waiting for transfers between devices: 81.3 us -> 93.8 us  [swap(): return lax.ppermute(value, axis, [(i, i ^ mask) for i in range(count)])]
    pallas_call x6, Pallas kernels: 37.8 us -> 29.9 us  [weight_blocks(): pl.pallas_call(kernel, in_specs=[pl.BlockSpec(memory_space=pltpu.SMEM)] +...]
    ppermute x27 -> x33, starting transfers between devices: 24.9 us -> 31.9 us  [swap(): return lax.ppermute(value, axis, [(i, i ^ mask) for i in range(count)])]
    dot_general x4 -> x2, matrix products: 14.1 us -> 7.62 us  [the longest x1 4.52 us: step(): lax.dot_general(after(gate_grad, done[0]), gate_w, COLS, preferred_elemen...]
    pallas_call x2 -> x1, Pallas kernels: 13.9 us -> 9.68 us  [hidden_grads(): pl.pallas_call(kernel, grid_spec=pltpu.PrefetchScalarGridSpec(num_scalar_...]
    add x6 -> x4, other arithmetic: 6 us -> 7.33 us  [advance(): rest = keep[middle:] + got[middle:].astype(F32)]
    unnamed x52 -> x44, local copies, waits for them, and re-layouts: 5.25 us -> 5.54 us
  transfers between devices with their start and end apart: 27 -> 33, of which waited for: 12 -> 16; matrix products, arithmetic and copies ran while one was open for 13% -> 11% of each run, Pallas kernels for 34% -> 26%
where the time goes in v2:
time: 218 us; the launch traced here: 217 us
  waiting for transfers between devices  93.8 us (43%)
  Pallas kernels  60.3 us (28%)
  starting transfers between devices  31.9 us (15%)
  other arithmetic  16.6 us (8%)
  matrix products  7.62 us (3%)
  local copies, waits for them, and re-layouts  5.81 us (3%)
    ppermute x33, waiting for transfers between devices, swap(): return lax.ppermute(value, axis, [(i, i ^ mask) for i in range(count)])  93.8 us
    ppermute x33, starting transfers between devices, swap(): return lax.ppermute(value, axis, [(i, i ^ mask) for i in range(count)])  31.9 us
    pallas_call x6, Pallas kernels, weight_blocks(): pl.pallas_call(kernel, in_specs=[pl.BlockSpec(memory_space=pltpu.SMEM)] +...  29.9 us
    pallas_call x2, Pallas kernels, activations(): pl.pallas_call(kernel, grid_spec=pltpu.PrefetchScalarGridSpec(num_scalar_...  15.5 us
    pallas_call x1, Pallas kernels, hidden_grads(): pl.pallas_call(kernel, grid_spec=pltpu.PrefetchScalarGridSpec(num_scalar_...  9.68 us
    add x4, other arithmetic, advance(): rest = keep[middle:] + got[middle:].astype(F32)  7.33 us
    unnamed x44, local copies, waits for them, and re-layouts  5.54 us
    pallas_call x2, Pallas kernels, pick_columns(): pl.pallas_call(kernel, grid_spec=pltpu.PrefetchScalarGridSpec(num_scalar_...  5.2 us
  transfers between devices with their start and end apart: 33, of which 16 were waited for; matrix products, arithmetic and copies ran while one was open for 11% of the time, Pallas kernels for 26%

profile of v2, /device:TPU:0, one launch (start us, length us, event | category | flops | bytes accessed | tf_op | source)
XLA Modules:
  0.0 216.9 jit_solution(4360916258186055180)
XLA Ops:
  1.2 2.6 %collective-permute-start.6 = (bf16[192,2048]{1,0:T(8,128)(2,1)}, bf16[192,2048]{1,0:T(8,128)(2,1)S(1)}, u32[]{:S(2)}, u32[]{:S(2)}) collective-permute-start(bf16[192,2048]{1,0:T(8,128)(2,1)} %refs_0_.7), channel_id=1, source_target_pairs={{0,2},{1,3},{2,0},{3,1},{4,6},{5,7},{6,4},{7,5},{8,10},{9,11},{10,... | collective-permute-start | bytes 2359304 | tf_op jit(solution)/shard_map/ppermute | solution.py:17
  7.5 7.8 %shard_map.112 = (f32[384,768]{1,0:T(8,128)}, f32[384,768]{1,0:T(8,128)}, bf16[384,768]{1,0:T(8,128)(2,1)}) custom-call(s32[2]{0:T(128)} %pad_add_fusion.scalar_ref.expert_ref, bf16[192,4]{1,0:T(8,128)(2,1)} %copy-done.10, bf16[192,4]{1,0:T(8,128)(2,1)} %copy-done.12, bf16[192,2048]{1,0:T(8,128)(2,1)} %refs_0_.7, bf16[192,2048]{1,0:T(8,128)(2,1)} %copy-done.19, ...), custom_call_target="tpu_custom_call" | custom-call | flops 2415919104 | bytes 6291456 | tf_op jit(solution)/shard_map/pallas_call | solution.py:84
  15.3 6.8 %collective-permute-done.6.refs_2_ = bf16[192,2048]{1,0:T(8,128)(2,1)S(1)} collective-permute-done((bf16[192,2048]{1,0:T(8,128)(2,1)}, bf16[192,2048]{1,0:T(8,128)(2,1)S(1)}, u32[]{:S(2)}, u32[]{:S(2)}) %collective-permute-start.6) | collective-permute-done | bytes 786464 | tf_op jit(solution)/shard_map/ppermute | solution.py:17
  22.1 2.6 %shard_map.110.refs_0_.refs_4_ = bf16[192,1024]{1,0:T(8,128)(2,1)} custom-call(s32[2]{0:T(128)} %pad_add_fusion.scalar_ref.expert_ref, bf16[192,2048]{1,0:T(8,128)(2,1)} %in_ref.3), custom_call_target="tpu_custom_call" | custom-call | tf_op jit(solution)/shard_map/pallas_call | solution.py:36
  24.7 1.7 collective-permute-start.5
  26.7 1.3 collective-permute-start.2
  28.6 9.4 %collective-permute-done.1.refs_0_.refs_2_ = bf16[192,4]{1,0:T(8,128)(2,1)S(1)} collective-permute-done((bf16[192,4]{1,0:T(8,128)(2,1)}, bf16[192,4]{1,0:T(8,128)(2,1)S(1)}, u32[]{:S(2)}, u32[]{:S(2)}) %collective-permute-start.1) | collective-permute-done | bytes 1568 | tf_op jit(solution)/shard_map/ppermute | solution.py:17
  39.6 7.7 %shard_map.113 = (f32[384,768]{1,0:T(8,128)}, f32[384,768]{1,0:T(8,128)}, bf16[384,768]{1,0:T(8,128)(2,1)}) custom-call(s32[2]{0:T(128)} %pad_add_fusion.scalar_ref.expert_ref, bf16[192,4]{1,0:T(8,128)(2,1)} %copy-done.13, bf16[192,4]{1,0:T(8,128)(2,1)} %copy-done.14, bf16[192,2048]{1,0:T(8,128)(2,1)} %copy-done.20, bf16[192,2048]{1,0:T(8,128)(2,1)} %copy-done.21, ...), custom_call_target="tpu_custom_call" | custom-call | flops 2415919104 | bytes 6291456 | tf_op jit(solution)/shard_map/pallas_call | solution.py:84
  47.7 1.4 collective-permute-done.10.refs_3_.refs_10_
  49.9 4.3 %shard_map.114 = bf16[4,768,256]{2,1,0:T(8,128)(2,1)} custom-call(s32[2]{0:T(128)} %pad_add_fusion.scalar_ref.expert_ref, bf16[192,1024]{1,0:T(8,128)(2,1)} %shard_map.110.refs_0_.refs_4_, bf16[192,1024]{1,0:T(8,128)(2,1)} %copy-done.8, bf16[192,1024]{1,0:T(8,128)(2,1)} %copy-done.7, bf16[192,1024]{1,0:T(8,128)(2,1)} %copy-done.9, ...), custom_call_target="tpu_custom_call" | custom-call | flops 1207959552 | bytes 1572864 | tf_op jit(solution)/shard_map/pallas_call | solution.py:202
  54.2 1.7 collective-permute-start.12
  55.9 2.6 %shard_map.111.refs_5_.refs_0_ = bf16[192,1024]{1,0:T(8,128)(2,1)} custom-call(s32[2]{0:T(128)} %pad_add_fusion.scalar_ref.expert_ref, bf16[192,2048]{1,0:T(8,128)(2,1)} %in_ref.3), custom_call_target="tpu_custom_call" | custom-call | tf_op jit(solution)/shard_map/pallas_call | solution.py:36
  58.5 1.5 collective-permute-start.9
  60.0 9.7 %collective-permute-done.9.refs_9_.refs_2_ = bf16[192,1024]{1,0:T(8,128)(2,1)S(1)} collective-permute-done((bf16[192,1024]{1,0:T(8,128)(2,1)}, bf16[192,1024]{1,0:T(8,128)(2,1)S(1)}, u32[]{:S(2)}, u32[]{:S(2)}) %collective-permute-start.9) | collective-permute-done | bytes 393248 | tf_op jit(solution)/shard_map/ppermute | solution.py:17
  69.8 1.7 collective-permute-done.11.refs_11_.refs_3_
  72.2 9.7 %shard_map.115 = (bf16[768,768]{1,0:T(8,128)(2,1)}, bf16[768,768]{1,0:T(8,128)(2,1)}, bf16[768,1]{1,0:T(8,128)(2,1)}) custom-call(s32[2]{0:T(128)} %pad_add_fusion.scalar_ref.expert_ref, bf16[192,4]{1,0:T(8,128)(2,1)} %copy-done.10, bf16[192,4]{1,0:T(8,128)(2,1)} %copy-done.12, bf16[192,4]{1,0:T(8,128)(2,1)} %copy-done.13, bf16[192,4]{1,0:T(8,128)(2,1)} %copy-done.14, ...), custom_call_target="tpu_custom_call" | custom-call | flops 2415919104 | bytes 3145728 | tf_op jit(solution)/shard_map/pallas_call | solution.py:152
  81.9 5.1 %shard_map.116 = (bf16[4,256,384]{2,1,0:T(8,128)(2,1)}, bf16[4,256,384]{2,1,0:T(8,128)(2,1)}) custom-call(s32[2]{0:T(128)} %pad_add_fusion.scalar_ref.expert_ref, bf16[192,2048]{1,0:T(8,128)(2,1)} %refs_0_.7, bf16[192,2048]{1,0:T(8,128)(2,1)} %copy-done.19, bf16[192,2048]{1,0:T(8,128)(2,1)} %copy-done.20, bf16[192,2048]{1,0:T(8,128)(2,1)} %copy-done.21, ...), custom_call_target="tpu_custom_call" | custom-call | flops 1207959552 | bytes 1572864 | tf_op jit(solution)/shard_map/pallas_call | solution.py:202
  87.0 1.5 collective-permute-start.13
  88.5 4.8 %shard_map.117 = (bf16[4,256,384]{2,1,0:T(8,128)(2,1)}, bf16[4,256,384]{2,1,0:T(8,128)(2,1)}) custom-call(s32[2]{0:T(128)} %pad_add_fusion.scalar_ref.expert_ref, bf16[192,2048]{1,0:T(8,128)(2,1)} %refs_0_.7, bf16[192,2048]{1,0:T(8,128)(2,1)} %copy-done.19, bf16[192,2048]{1,0:T(8,128)(2,1)} %copy-done.20, bf16[192,2048]{1,0:T(8,128)(2,1)} %copy-done.21, ...), custom_call_target="tpu_custom_call" | custom-call | flops 1207959552 | bytes 1572864 | tf_op jit(solution)/shard_map/pallas_call | solution.py:202
  93.9 1.5 collective-permute-start.20
  96.0 4.8 %shard_map.118 = f32[4,768,256]{2,1,0:T(8,128)} custom-call(s32[2]{0:T(128)} %pad_add_fusion.scalar_ref.expert_ref, bf16[192,1024]{1,0:T(8,128)(2,1)} %shard_map.111.refs_5_.refs_0_, bf16[192,1024]{1,0:T(8,128)(2,1)} %copy-done.1, bf16[192,1024]{1,0:T(8,128)(2,1)} %copy-done, bf16[192,1024]{1,0:T(8,128)(2,1)} %copy-done.2, ...), custom_call_target="tpu_custom_call" | custom-call | flops 1207959552 | bytes 1572864 | tf_op jit(solution)/shard_map/pallas_call | solution.py:202
  100.7 3.5 %slice_add_fusion = (f32[2,768,256]{2,1,0:T(8,128)S(1)}, bf16[2,768,256]{2,1,0:T(8,128)(2,1)}) fusion(f32[4,768,256]{2,1,0:T(8,128)} %shard_map.118, bf16[4,768,256]{2,1,0:T(8,128)(2,1)} %collective-permute-done.12), kind=kLoop, calls=%fused_computation.1 | loop fusion | flops 1966080 | bytes 7077888 | tf_op jit(solution)/shard_map/add | solution.py:319
  104.3 5.5 %shard_map.119 = (f32[4,256,384]{2,1,0:T(8,128)}, f32[4,256,384]{2,1,0:T(8,128)}) custom-call(s32[2]{0:T(128)} %pad_add_fusion.scalar_ref.expert_ref, bf16[192,2048]{1,0:T(8,128)(2,1)} %refs_0_.7, bf16[192,2048]{1,0:T(8,128)(2,1)} %copy-done.19, bf16[192,2048]{1,0:T(8,128)(2,1)} %copy-done.20, bf16[192,2048]{1,0:T(8,128)(2,1)} %copy-done.21, ...), custom_call_target="tpu_custom_call" | custom-call | flops 1207959552 | bytes 1572864 | tf_op jit(solution)/shard_map/pallas_call | solution.py:202
  110.7 1.7 convert_add_fusion
  112.4 5.4 %shard_map.120 = (f32[4,256,384]{2,1,0:T(8,128)}, f32[4,256,384]{2,1,0:T(8,128)}) custom-call(s32[2]{0:T(128)} %pad_add_fusion.scalar_ref.expert_ref, bf16[192,2048]{1,0:T(8,128)(2,1)} %refs_0_.7, bf16[192,2048]{1,0:T(8,128)(2,1)} %copy-done.19, bf16[192,2048]{1,0:T(8,128)(2,1)} %copy-done.20, bf16[192,2048]{1,0:T(8,128)(2,1)} %copy-done.21, ...), custom_call_target="tpu_custom_call" | custom-call | flops 1207959552 | bytes 1572864 | tf_op jit(solution)/shard_map/pallas_call | solution.py:202
  117.8 1.9 convert_add_fusion.2
  120.1 1.7 collective-permute-start.22
  121.8 4.5 %fusion.21 = f32[768,2048]{1,0:T(8,128)S(1)} fusion(bf16[768,768]{1,0:T(8,128)(2,1)S(1)} %copy-done.18, bf16[1,2048,768]{2,1,0:T(8,128)(2,1)} %param.11), kind=kOutput, calls=%fused_computation.57 | convolution fusion | flops 2415919104 | bytes 10616832 | tf_op jit(solution)/shard_map/dot_general | solution.py:336
  126.3 3.1 %add_convert_fusion = bf16[768,2048]{1,0:T(8,128)(2,1)S(1)} fusion(f32[768,2048]{1,0:T(8,128)S(1)} %fusion.21, bf16[768,768]{1,0:T(8,128)(2,1)S(1)} %copy-done.17, bf16[1,2048,768]{2,1,0:T(8,128)(2,1)S(1)} %copy-done.16), kind=kOutput, calls=%fused_computation | convolution fusion | flops 2419064832 | bytes 13762560 | tf_op jit(solution)/shard_map/dot_general | solution.py:337
  130.5 9.7 %collective-permute-done.16 = bf16[2,768,256]{2,1,0:T(8,128)(2,1)S(1)} collective-permute-done((bf16[2,768,256]{2,1,0:T(8,128)(2,1)S(1)}, bf16[2,768,256]{2,1,0:T(8,128)(2,1)S(1)}, u32[]{:S(2)}, u32[]{:S(2)}) %collective-permute-start.16) | collective-permute-done | bytes 786464 | tf_op jit(solution)/shard_map/ppermute | solution.py:17
  140.3 1.5 collective-permute-start.28
  141.9 1.3 add_convert_fusion.4
  143.2 3.5 %collective-permute-done.22 = bf16[2,256,384]{2,1,0:T(8,128)(2,1)S(1)} collective-permute-done((bf16[2,256,384]{2,1,0:T(8,128)(2,1)S(1)}, bf16[2,256,384]{2,1,0:T(8,128)(2,1)S(1)}, u32[]{:S(2)}, u32[]{:S(2)}) %collective-permute-start.22) | collective-permute-done | bytes 393248 | tf_op jit(solution)/shard_map/ppermute | solution.py:17
  146.7 1.6 collective-permute-start.24
  149.1 10.5 %collective-permute-done.21 = bf16[2,256,384]{2,1,0:T(8,128)(2,1)S(1)} collective-permute-done((bf16[2,256,384]{2,1,0:T(8,128)(2,1)S(1)}, bf16[2,256,384]{2,1,0:T(8,128)(2,1)S(1)}, u32[]{:S(2)}, u32[]{:S(2)}) %collective-permute-start.21) | collective-permute-done | bytes 393248 | tf_op jit(solution)/shard_map/ppermute | solution.py:17
  159.6 1.1 collective-permute-start.18
  160.9 2.7 %collective-permute-start.32 = (bf16[1,768,256]{2,1,0:T(8,128)(2,1)S(1)}, bf16[1,768,256]{2,1,0:T(8,128)(2,1)S(1)}, u32[]{:S(2)}, u32[]{:S(2)}) collective-permute-start(bf16[1,768,256]{2,1,0:T(8,128)(2,1)S(1)} %fusion.3), channel_id=1, source_target_pairs={{0,16},{4,20},{8,24},{12,28},{16,0},{20,4},{24,8},{28,12},{1,17},{... | collective-permute-start | bytes 1179656 | tf_op jit(solution)/shard_map/ppermute | solution.py:17
  164.4 2.6 %collective-permute-start.29 = (bf16[1,256,384]{2,1,0:T(8,128)(2,1)S(1)}, bf16[1,256,384]{2,1,0:T(8,128)(2,1)S(1)}, u32[]{:S(2)}, u32[]{:S(2)}) collective-permute-start(bf16[1,256,384]{2,1,0:T(8,128)(2,1)S(1)} %fusion.15), channel_id=1, source_target_pairs={{0,16},{4,20},{8,24},{12,28},{16,0},{20,4},{24,8},{28,12},{1,17},{... | collective-permute-start | bytes 589832 | tf_op jit(solution)/shard_map/ppermute | solution.py:17
  167.9 12.1 %collective-permute-done.18 = bf16[192,2048]{1,0:T(8,128)(2,1)S(1)} collective-permute-done((bf16[192,2048]{1,0:T(8,128)(2,1)S(1)}, bf16[192,2048]{1,0:T(8,128)(2,1)S(1)}, u32[]{:S(2)}, u32[]{:S(2)}) %collective-permute-start.18) | collective-permute-done | bytes 786464 | tf_op jit(solution)/shard_map/ppermute | solution.py:17
  180.0 2.6 %collective-permute-start.30 = (bf16[1,256,384]{2,1,0:T(8,128)(2,1)S(1)}, bf16[1,256,384]{2,1,0:T(8,128)(2,1)S(1)}, u32[]{:S(2)}, u32[]{:S(2)}) collective-permute-start(bf16[1,256,384]{2,1,0:T(8,128)(2,1)S(1)} %fusion.10), channel_id=1, source_target_pairs={{0,16},{4,20},{8,24},{12,28},{16,0},{20,4},{24,8},{28,12},{1,17},{... | collective-permute-start | bytes 589832 | tf_op jit(solution)/shard_map/ppermute | solution.py:17
  182.6 1.3 add_convert_fusion.1
  183.9 1.9 collective-permute-done.27
  185.8 1.4 collective-permute-start.31
  187.2 16.0 %collective-permute-done.26 = bf16[1,256,384]{2,1,0:T(8,128)(2,1)S(1)} collective-permute-done((bf16[1,256,384]{2,1,0:T(8,128)(2,1)S(1)}, bf16[1,256,384]{2,1,0:T(8,128)(2,1)S(1)}, u32[]{:S(2)}, u32[]{:S(2)}) %collective-permute-start.26) | collective-permute-done | bytes 196640 | tf_op jit(solution)/shard_map/ppermute | solution.py:17
  203.2 1.0 fusion.2
  204.2 3.2 %collective-permute-done.29 = bf16[1,256,384]{2,1,0:T(8,128)(2,1)S(1)} collective-permute-done((bf16[1,256,384]{2,1,0:T(8,128)(2,1)S(1)}, bf16[1,256,384]{2,1,0:T(8,128)(2,1)S(1)}, u32[]{:S(2)}, u32[]{:S(2)}) %collective-permute-start.29) | collective-permute-done | bytes 196640 | tf_op jit(solution)/shard_map/ppermute | solution.py:17
  207.6 4.1 %collective-permute-done.30 = bf16[1,256,384]{2,1,0:T(8,128)(2,1)S(1)} collective-permute-done((bf16[1,256,384]{2,1,0:T(8,128)(2,1)S(1)}, bf16[1,256,384]{2,1,0:T(8,128)(2,1)S(1)}, u32[]{:S(2)}, u32[]{:S(2)}) %collective-permute-start.30) | collective-permute-done | bytes 196640 | tf_op jit(solution)/shard_map/ppermute | solution.py:17
  212.6 3.3 %collective-permute-done.31 = bf16[1,256,384]{2,1,0:T(8,128)(2,1)S(1)} collective-permute-done((bf16[1,256,384]{2,1,0:T(8,128)(2,1)S(1)}, bf16[1,256,384]{2,1,0:T(8,128)(2,1)S(1)}, u32[]{:S(2)}, u32[]{:S(2)}) %collective-permute-start.31) | collective-permute-done | bytes 196640 | tf_op jit(solution)/shard_map/ppermute | solution.py:17
  (102 shorter events, 17.1 us)
Async XLA Ops:
  0.6 6.0 %collective-permute-start.7 = (bf16[192,2048]{1,0:T(8,128)(2,1)}, bf16[192,2048]{1,0:T(8,128)(2,1)S(1)}, u32[]{:S(2)}, u32[]{:S(2)}) collective-permute-start(bf16[192,2048]{1,0:T(8,128)(2,1)} %refs_0_.7), channel_id=1, source_target_pairs={{0,1},{1,0},{2,3},{3,2},{4,5},{5,4},{6,7},{7,6},{8,9},{9,8},{10,11... | collective-permute-start | bytes 2359304 | tf_op jit(solution)/shard_map/ppermute | solution.py:17
  1.2 20.9 %collective-permute-start.6 = (bf16[192,2048]{1,0:T(8,128)(2,1)}, bf16[192,2048]{1,0:T(8,128)(2,1)S(1)}, u32[]{:S(2)}, u32[]{:S(2)}) collective-permute-start(bf16[192,2048]{1,0:T(8,128)(2,1)} %refs_0_.7), channel_id=1, source_target_pairs={{0,2},{1,3},{2,0},{3,1},{4,6},{5,7},{6,4},{7,5},{8,10},{9,11},{10,... | collective-permute-start | bytes 2359304 | tf_op jit(solution)/shard_map/ppermute | solution.py:17
  5.3 1.3 copy-start.10
  5.3 1.3 collective-permute-start
  22.1 16.0 %copy-start.20 = (bf16[192,2048]{1,0:T(8,128)(2,1)}, bf16[192,2048]{1,0:T(8,128)(2,1)S(1)}, u32[]{:S(2)}) copy-start(bf16[192,2048]{1,0:T(8,128)(2,1)S(1)} %collective-permute-done.6.refs_2_) | copy-start | bytes 2359300
  22.1 16.0 %collective-permute-start.8 = (bf16[192,2048]{1,0:T(8,128)(2,1)S(1)}, bf16[192,2048]{1,0:T(8,128)(2,1)S(1)}, u32[]{:S(2)}, u32[]{:S(2)}) collective-permute-start(bf16[192,2048]{1,0:T(8,128)(2,1)S(1)} %collective-permute-done.6.refs_2_), channel_id=1, source_target_pairs={{0,1},{1,0},{2,3},{3,2},{4,5},{5,4},{6,7},{7,6},{8,9},{9,8},{10,11... | collective-permute-start | bytes 2359304 | tf_op jit(solution)/shard_map/ppermute | solution.py:17
  24.7 22.6 %collective-permute-start.5 = (bf16[192,1024]{1,0:T(8,128)(2,1)}, bf16[192,1024]{1,0:T(8,128)(2,1)S(1)}, u32[]{:S(2)}, u32[]{:S(2)}) collective-permute-start(bf16[192,1024]{1,0:T(8,128)(2,1)} %shard_map.110.refs_0_.refs_4_), channel_id=1, source_target_pairs={{0,2},{1,3},{2,0},{3,1},{4,6},{5,7},{6,4},{7,5},{8,10},{9,11},{10,... | collective-permute-start | bytes 1179656 | tf_op jit(solution)/shard_map/ppermute | solution.py:17
  26.5 11.5 %collective-permute-start.1 = (bf16[192,4]{1,0:T(8,128)(2,1)}, bf16[192,4]{1,0:T(8,128)(2,1)S(1)}, u32[]{:S(2)}, u32[]{:S(2)}) collective-permute-start(bf16[192,4]{1,0:T(8,128)(2,1)} %copy-done.10), channel_id=1, source_target_pairs={{0,2},{1,3},{2,0},{3,1},{4,6},{5,7},{6,4},{7,5},{8,10},{9,11},{10,... | collective-permute-start | bytes 4616 | tf_op jit(solution)/shard_map/ppermute | solution.py:17
  26.7 11.4 %collective-permute-start.2 = (bf16[192,4]{1,0:T(8,128)(2,1)}, bf16[192,4]{1,0:T(8,128)(2,1)S(1)}, u32[]{:S(2)}, u32[]{:S(2)}) collective-permute-start(bf16[192,4]{1,0:T(8,128)(2,1)} %copy-done.10), channel_id=1, source_target_pairs={{0,3},{1,2},{2,1},{3,0},{4,7},{5,6},{6,5},{7,4},{8,11},{9,10},{10,... | collective-permute-start | bytes 4616 | tf_op jit(solution)/shard_map/ppermute | solution.py:17
  28.0 19.7 %collective-permute-start.3 = (bf16[192,1024]{1,0:T(8,128)(2,1)}, bf16[192,1024]{1,0:T(8,128)(2,1)S(1)}, u32[]{:S(2)}, u32[]{:S(2)}) collective-permute-start(bf16[192,1024]{1,0:T(8,128)(2,1)} %shard_map.110.refs_0_.refs_4_), channel_id=1, source_target_pairs={{0,1},{1,0},{2,3},{3,2},{4,5},{5,4},{6,7},{7,6},{8,9},{9,8},{10,11... | collective-permute-start | bytes 1179656 | tf_op jit(solution)/shard_map/ppermute | solution.py:17
  47.3 1.8 copy-start.7
  47.4 1.8 collective-permute-start.10
  47.7 1.4 copy-start.8
  54.2 46.5 %collective-permute-start.12 = (bf16[4,768,256]{2,1,0:T(8,128)(2,1)}, bf16[4,768,256]{2,1,0:T(8,128)(2,1)}, u32[]{:S(2)}, u32[]{:S(2)}) collective-permute-start(bf16[4,768,256]{2,1,0:T(8,128)(2,1)} %shard_map.114), channel_id=1, source_target_pairs={{0,4},{4,0},{8,12},{12,8},{16,20},{20,16},{24,28},{28,24},{1,5},{5... | collective-permute-start | bytes 4718600 | tf_op jit(solution)/shard_map/ppermute | solution.py:17
  58.5 11.2 %collective-permute-start.9 = (bf16[192,1024]{1,0:T(8,128)(2,1)}, bf16[192,1024]{1,0:T(8,128)(2,1)S(1)}, u32[]{:S(2)}, u32[]{:S(2)}) collective-permute-start(bf16[192,1024]{1,0:T(8,128)(2,1)} %shard_map.111.refs_5_.refs_0_), channel_id=1, source_target_pairs={{0,2},{1,3},{2,0},{3,1},{4,6},{5,7},{6,4},{7,5},{8,10},{9,11},{10,... | collective-permute-start | bytes 1179656 | tf_op jit(solution)/shard_map/ppermute | solution.py:17
  60.0 9.7 %collective-permute-start.4 = (bf16[192,1024]{1,0:T(8,128)(2,1)}, bf16[192,1024]{1,0:T(8,128)(2,1)S(1)}, u32[]{:S(2)}, u32[]{:S(2)}) collective-permute-start(bf16[192,1024]{1,0:T(8,128)(2,1)} %shard_map.111.refs_5_.refs_0_), channel_id=1, source_target_pairs={{0,1},{1,0},{2,3},{3,2},{4,5},{5,4},{6,7},{7,6},{8,9},{9,8},{10,11... | collective-permute-start | bytes 1179656 | tf_op jit(solution)/shard_map/ppermute | solution.py:17
  69.8 1.7 copy-start
  69.8 1.7 collective-permute-start.11
  69.8 1.7 copy-start.1
  87.0 22.8 %collective-permute-start.13 = (bf16[4,256,384]{2,1,0:T(8,128)(2,1)}, bf16[4,256,384]{2,1,0:T(8,128)(2,1)S(1)}, u32[]{:S(2)}, u32[]{:S(2)}) collective-permute-start(bf16[4,256,384]{2,1,0:T(8,128)(2,1)} %get-tuple-element.68), channel_id=1, source_target_pairs={{0,8},{4,12},{8,0},{12,4},{16,24},{20,28},{24,16},{28,20},{1,9},{5... | collective-permute-start | bytes 2359304 | tf_op jit(solution)/shard_map/ppermute | solution.py:17
  93.4 24.4 %collective-permute-start.14 = (bf16[4,256,384]{2,1,0:T(8,128)(2,1)}, bf16[4,256,384]{2,1,0:T(8,128)(2,1)}, u32[]{:S(2)}, u32[]{:S(2)}) collective-permute-start(bf16[4,256,384]{2,1,0:T(8,128)(2,1)} %get-tuple-element.70), channel_id=1, source_target_pairs={{0,4},{4,0},{8,12},{12,8},{16,20},{20,16},{24,28},{28,24},{1,5},{5... | collective-permute-start | bytes 2359304 | tf_op jit(solution)/shard_map/ppermute | solution.py:17
  93.9 46.4 %collective-permute-start.20 = (bf16[4,256,384]{2,1,0:T(8,128)(2,1)}, bf16[4,256,384]{2,1,0:T(8,128)(2,1)}, u32[]{:S(2)}, u32[]{:S(2)}) collective-permute-start(bf16[4,256,384]{2,1,0:T(8,128)(2,1)} %get-tuple-element.87), channel_id=1, source_target_pairs={{0,4},{4,0},{8,12},{12,8},{16,20},{20,16},{24,28},{28,24},{1,5},{5... | collective-permute-start | bytes 2359304 | tf_op jit(solution)/shard_map/ppermute | solution.py:17
  95.4 64.2 %collective-permute-start.19 = (bf16[4,256,384]{2,1,0:T(8,128)(2,1)}, bf16[4,256,384]{2,1,0:T(8,128)(2,1)S(1)}, u32[]{:S(2)}, u32[]{:S(2)}) collective-permute-start(bf16[4,256,384]{2,1,0:T(8,128)(2,1)} %get-tuple-element.86), channel_id=1, source_target_pairs={{0,4},{4,0},{8,12},{12,8},{16,20},{20,16},{24,28},{28,24},{1,5},{5... | collective-permute-start | bytes 2359304 | tf_op jit(solution)/shard_map/ppermute | solution.py:17
  109.8 0.9 copy-start.6
  117.8 1.9 copy-start.5
  117.8 4.0 %copy-start.18 = (bf16[768,768]{1,0:T(8,128)(2,1)S(1)}, bf16[768,768]{1,0:T(8,128)(2,1)}, u32[]{:S(2)}) copy-start(bf16[768,768]{1,0:T(8,128)(2,1)} %get-tuple-element.81.refs_4_) | copy-start | bytes 3538948
  119.7 6.6 %copy-start.16 = (bf16[1,2048,768]{2,1,0:T(8,128)(2,1)S(1)}, bf16[1,2048,768]{2,1,0:T(8,128)(2,1)}, u32[]{:S(2)}) copy-start(bf16[1,2048,768]{2,1,0:T(8,128)(2,1)} %param.12) | copy-start | bytes 9437188
  119.7 6.6 %copy-start.17 = (bf16[768,768]{1,0:T(8,128)(2,1)S(1)}, bf16[768,768]{1,0:T(8,128)(2,1)}, u32[]{:S(2)}) copy-start(bf16[768,768]{1,0:T(8,128)(2,1)} %get-tuple-element.82.refs_4_) | copy-start | bytes 3538948
  119.7 20.5 %collective-permute-start.16 = (bf16[2,768,256]{2,1,0:T(8,128)(2,1)S(1)}, bf16[2,768,256]{2,1,0:T(8,128)(2,1)S(1)}, u32[]{:S(2)}, u32[]{:S(2)}) collective-permute-start(bf16[2,768,256]{2,1,0:T(8,128)(2,1)S(1)} %copy-done.5), channel_id=1, source_target_pairs={{0,8},{4,12},{8,0},{12,4},{16,24},{20,28},{24,16},{28,20},{1,9},{5... | collective-permute-start | bytes 2359304 | tf_op jit(solution)/shard_map/ppermute | solution.py:17
  120.1 26.6 %collective-permute-start.22 = (bf16[2,256,384]{2,1,0:T(8,128)(2,1)S(1)}, bf16[2,256,384]{2,1,0:T(8,128)(2,1)S(1)}, u32[]{:S(2)}, u32[]{:S(2)}) collective-permute-start(bf16[2,256,384]{2,1,0:T(8,128)(2,1)S(1)} %get-tuple-element.114), channel_id=1, source_target_pairs={{0,8},{4,12},{8,0},{12,4},{16,24},{20,28},{24,16},{28,20},{1,9},{5... | collective-permute-start | bytes 1179656 | tf_op jit(solution)/shard_map/ppermute | solution.py:17
  129.4 0.9 copy-start.11
  129.6 12.3 %copy-start.4 = (f32[4,256,384]{2,1,0:T(8,128)S(1)}, f32[4,256,384]{2,1,0:T(8,128)}, u32[]{:S(2)}) copy-start(f32[4,256,384]{2,1,0:T(8,128)} %get-tuple-element.79) | copy-start | bytes 4718596
  129.6 17.1 %collective-permute-start.15 = (bf16[192,2048]{1,0:T(8,128)(2,1)S(1)}, bf16[192,2048]{1,0:T(8,128)(2,1)S(1)}, u32[]{:S(2)}, u32[]{:S(2)}) collective-permute-start(bf16[192,2048]{1,0:T(8,128)(2,1)S(1)} %get-tuple-element.107), channel_id=1, source_target_pairs={{0,1},{1,0},{2,3},{3,2},{4,5},{5,4},{6,7},{7,6},{8,9},{9,8},{10,11... | collective-permute-start | bytes 2359304 | tf_op jit(solution)/shard_map/ppermute | solution.py:17
  140.2 8.1 %collective-permute-start.17 = (bf16[192,2048]{1,0:T(8,128)(2,1)S(1)}, bf16[192,2048]{1,0:T(8,128)(2,1)S(1)}, u32[]{:S(2)}, u32[]{:S(2)}) collective-permute-start(bf16[192,2048]{1,0:T(8,128)(2,1)S(1)} %get-tuple-element.108), channel_id=1, source_target_pairs={{0,1},{1,0},{2,3},{3,2},{4,5},{5,4},{6,7},{7,6},{8,9},{9,8},{10,11... | collective-permute-start | bytes 2359304 | tf_op jit(solution)/shard_map/ppermute | solution.py:17
  140.3 20.6 %collective-permute-start.28 = (bf16[2,256,384]{2,1,0:T(8,128)(2,1)S(1)}, bf16[2,256,384]{2,1,0:T(8,128)(2,1)S(1)}, u32[]{:S(2)}, u32[]{:S(2)}) collective-permute-start(bf16[2,256,384]{2,1,0:T(8,128)(2,1)S(1)} %get-tuple-element.110), channel_id=1, source_target_pairs={{0,4},{4,0},{8,12},{12,8},{16,20},{20,16},{24,28},{28,24},{1,5},{5... | collective-permute-start | bytes 1179656 | tf_op jit(solution)/shard_map/ppermute | solution.py:17
  146.7 16.9 %collective-permute-start.23 = (bf16[192,1]{1,0:T(8,128)(2,1)S(1)}, bf16[192,1]{1,0:T(8,128)(2,1)S(1)}, u32[]{:S(2)}, u32[]{:S(2)}) collective-permute-start(bf16[192,1]{1,0:T(8,128)(2,1)S(1)} %get-tuple-element.117), channel_id=1, source_target_pairs={{0,1},{1,0},{2,3},{3,2},{4,5},{5,4},{6,7},{7,6},{8,9},{9,8},{10,11... | collective-permute-start | bytes 1160 | tf_op jit(solution)/shard_map/ppermute | solution.py:17
  146.7 14.0 %copy-start.3 = (f32[4,256,384]{2,1,0:T(8,128)S(1)}, f32[4,256,384]{2,1,0:T(8,128)}, u32[]{:S(2)}) copy-start(f32[4,256,384]{2,1,0:T(8,128)} %get-tuple-element.75) | copy-start | bytes 4718596
  146.7 17.2 %collective-permute-start.24 = (bf16[192,1]{1,0:T(8,128)(2,1)S(1)}, bf16[192,1]{1,0:T(8,128)(2,1)S(1)}, u32[]{:S(2)}, u32[]{:S(2)}) collective-permute-start(bf16[192,1]{1,0:T(8,128)(2,1)S(1)} %get-tuple-element.119), channel_id=1, source_target_pairs={{0,2},{1,3},{2,0},{3,1},{4,6},{5,7},{6,4},{7,5},{8,10},{9,11},{10,... | collective-permute-start | bytes 1160 | tf_op jit(solution)/shard_map/ppermute | solution.py:17
  148.3 11.2 %collective-permute-start.21 = (bf16[2,256,384]{2,1,0:T(8,128)(2,1)S(1)}, bf16[2,256,384]{2,1,0:T(8,128)(2,1)S(1)}, u32[]{:S(2)}, u32[]{:S(2)}) collective-permute-start(bf16[2,256,384]{2,1,0:T(8,128)(2,1)S(1)} %get-tuple-element.115), channel_id=1, source_target_pairs={{0,8},{4,12},{8,0},{12,4},{16,24},{20,28},{24,16},{28,20},{1,9},{5... | collective-permute-start | bytes 1179656 | tf_op jit(solution)/shard_map/ppermute | solution.py:17
  159.6 4.9 %collective-permute-start.25 = (bf16[192,1]{1,0:T(8,128)(2,1)S(1)}, bf16[192,1]{1,0:T(8,128)(2,1)S(1)}, u32[]{:S(2)}, u32[]{:S(2)}) collective-permute-start(bf16[192,1]{1,0:T(8,128)(2,1)S(1)} %get-tuple-element.118), channel_id=1, source_target_pairs={{0,3},{1,2},{2,1},{3,0},{4,7},{5,6},{6,5},{7,4},{8,11},{9,10},{10,... | collective-permute-start | bytes 1160 | tf_op jit(solution)/shard_map/ppermute | solution.py:17
  159.6 7.6 %copy-start.15 = (s32[192,2]{0,1:T(2,128)S(1)}, s32[192,2]{0,1:T(2,128)}, u32[]{:S(2)}) copy-start(s32[192,2]{0,1:T(2,128)} %param.9) | copy-start | bytes 4612
  159.6 20.4 %collective-permute-start.18 = (bf16[192,2048]{1,0:T(8,128)(2,1)S(1)}, bf16[192,2048]{1,0:T(8,128)(2,1)S(1)}, u32[]{:S(2)}, u32[]{:S(2)}) collective-permute-start(bf16[192,2048]{1,0:T(8,128)(2,1)S(1)} %add_convert_fusion.2), channel_id=1, source_target_pairs={{0,2},{1,3},{2,0},{3,1},{4,6},{5,7},{6,4},{7,5},{8,10},{9,11},{10,... | collective-permute-start | bytes 2359304 | tf_op jit(solution)/shard_map/ppermute | solution.py:17
  160.9 26.3 %collective-permute-start.32 = (bf16[1,768,256]{2,1,0:T(8,128)(2,1)S(1)}, bf16[1,768,256]{2,1,0:T(8,128)(2,1)S(1)}, u32[]{:S(2)}, u32[]{:S(2)}) collective-permute-start(bf16[1,768,256]{2,1,0:T(8,128)(2,1)S(1)} %fusion.3), channel_id=1, source_target_pairs={{0,16},{4,20},{8,24},{12,28},{16,0},{20,4},{24,8},{28,12},{1,17},{... | collective-permute-start | bytes 1179656 | tf_op jit(solution)/shard_map/ppermute | solution.py:17
  163.6 39.6 %collective-permute-start.26 = (bf16[1,256,384]{2,1,0:T(8,128)(2,1)S(1)}, bf16[1,256,384]{2,1,0:T(8,128)(2,1)S(1)}, u32[]{:S(2)}, u32[]{:S(2)}) collective-permute-start(bf16[1,256,384]{2,1,0:T(8,128)(2,1)S(1)} %fusion.14), channel_id=1, source_target_pairs={{0,16},{4,20},{8,24},{12,28},{16,0},{20,4},{24,8},{28,12},{1,17},{... | collective-permute-start | bytes 589832 | tf_op jit(solution)/shard_map/ppermute | solution.py:17
  163.9 21.9 %collective-permute-start.27 = (bf16[2,256,384]{2,1,0:T(8,128)(2,1)S(1)}, bf16[2,256,384]{2,1,0:T(8,128)(2,1)S(1)}, u32[]{:S(2)}, u32[]{:S(2)}) collective-permute-start(bf16[2,256,384]{2,1,0:T(8,128)(2,1)S(1)} %get-tuple-element.112), channel_id=1, source_target_pairs={{0,8},{4,12},{8,0},{12,4},{16,24},{20,28},{24,16},{28,20},{1,9},{5... | collective-permute-start | bytes 1179656 | tf_op jit(solution)/shard_map/ppermute | solution.py:17
  164.4 43.0 %collective-permute-start.29 = (bf16[1,256,384]{2,1,0:T(8,128)(2,1)S(1)}, bf16[1,256,384]{2,1,0:T(8,128)(2,1)S(1)}, u32[]{:S(2)}, u32[]{:S(2)}) collective-permute-start(bf16[1,256,384]{2,1,0:T(8,128)(2,1)S(1)} %fusion.15), channel_id=1, source_target_pairs={{0,16},{4,20},{8,24},{12,28},{16,0},{20,4},{24,8},{28,12},{1,17},{... | collective-permute-start | bytes 589832 | tf_op jit(solution)/shard_map/ppermute | solution.py:17
  180.0 31.6 %collective-permute-start.30 = (bf16[1,256,384]{2,1,0:T(8,128)(2,1)S(1)}, bf16[1,256,384]{2,1,0:T(8,128)(2,1)S(1)}, u32[]{:S(2)}, u32[]{:S(2)}) collective-permute-start(bf16[1,256,384]{2,1,0:T(8,128)(2,1)S(1)} %fusion.10), channel_id=1, source_target_pairs={{0,16},{4,20},{8,24},{12,28},{16,0},{20,4},{24,8},{28,12},{1,17},{... | collective-permute-start | bytes 589832 | tf_op jit(solution)/shard_map/ppermute | solution.py:17
  185.8 30.0 %collective-permute-start.31 = (bf16[1,256,384]{2,1,0:T(8,128)(2,1)S(1)}, bf16[1,256,384]{2,1,0:T(8,128)(2,1)S(1)}, u32[]{:S(2)}, u32[]{:S(2)}) collective-permute-start(bf16[1,256,384]{2,1,0:T(8,128)(2,1)S(1)} %fusion.11), channel_id=1, source_target_pairs={{0,16},{4,20},{8,24},{12,28},{16,0},{20,4},{24,8},{28,12},{1,17},{... | collective-permute-start | bytes 589832 | tf_op jit(solution)/shard_map/ppermute | solution.py:17
  (7 other events, 5.1 us)
